TPU v7x, 256 devices: a whole 4x4x8 slice. The times are simulated.
256 devices in a mesh: row: 32 (over z, x_hi, core), col: 8 (over y, x_lo).
Axes of the slice: x: 4 (x_hi: 2, x_lo: 2; x = x_hi * 2 + x_lo), y: 4, z: 8, core: 2. Of those that a mesh axis runs over, the one named last changes fastest.
Arguments:
- queries: bfloat16 [262144, 256], P(('row', 'col')), may hold values from -6 to 6
- documents: bfloat16 [8192, 256], P(('row', 'col')), may hold values from -6 to 6
- log_norms: float32 [262144], P(('row', 'col')), may hold values from 7 to 11
- weights: float32 [262144], P(('row', 'col')), may hold values from 1 to 10
- positives: int32 [262144], P(('row', 'col')), may hold values from 0 to 8191
Outputs:
- grad_queries: bfloat16 [262144, 256], P(('row', 'col'))
- grad_documents: bfloat16 [8192, 256], P(('row', 'col'))
- loss: float32 [], replicated
All inputs are finite; a program needn't handle non-finite values.
Results may differ from a plain program's by a relative error of at most 0.001.
The roundings to bfloat16 on the way count: a program that leaves them out, or rounds other values in their place, can miss the bound.
Values may be sent and summed in bfloat16 or wider, within the bound.
No kernel may reach another device: no remote copies, remote signals or barrier semaphores. Data moves between devices by JAX's collectives and lax.ppermute only.
A program may use at most 128 MiB of HBM per device.

v0:
```python
import functools
import itertools
import math

import jax
import jax.numpy as jnp
from jax import lax
from jax.experimental import pallas as pl
from jax.experimental.pallas import tpu as pltpu
from jax.sharding import Mesh
from jax.sharding import PartitionSpec as P


AXES = ("z", "xh", "core", "y", "xl")
X = ("xh", "xl")
Y = ("y",)
CHIPS = ("xh", "core", "y", "xl")
F32 = jnp.float32
BF16 = jnp.bfloat16
LOG2E = math.log2(math.e)
QT = 512
SUB = 256
SIDES = (0, 1, -1, 2)
TURNS = ((0, 0, 4), (2, 0, 4), (-1, 0, 4), (1, 0, 2), (1, 2, 4))
VMEM_LIMIT = 16 << 20


def other_core(array):
    return lax.ppermute(array, "core", [(0, 1), (1, 0)])


def moved(array, along, distance):
    if distance == 0:
        return array
    n_xh, n_y, n_xl = (lax.axis_size(axis) for axis in ("xh", "y", "xl"))
    n_x = n_xh * n_xl

    def at(x, core, y):
        return ((x // n_xl * 2 + core) * n_y + y) * n_xl + x % n_xl

    route = []
    for x, core, y in itertools.product(range(n_x), range(2), range(n_y)):
        in_x = along == (core == 0)
        to = ((x + distance) % n_x, y) if in_x else (x, (y + distance) % n_y)
        route.append((at(x, core, y), at(to[0], core, to[1])))
    return lax.ppermute(array, CHIPS, route)


def lay_out(own_ref, other_ref, rows_ref, other_rows_ref, q_ref, qt_ref, off_ref, w_ref, pos_ref, sem):
    n = own_ref.shape[0]
    own = pltpu.make_async_copy(own_ref, q_ref.at[:n], sem)
    own.start()
    for i, ref in enumerate((rows_ref, other_rows_ref)):
        part = slice(i * n, (i + 1) * n)
        w_ref[:, part] = ref[1:2, :]
        off_ref[:, part] = ref[0:1, :] * LOG2E - jnp.log2(ref[1:2, :])
        pos_ref[:, part] = ref[2:3, :].astype(jnp.int32)
    q_ref[n:, :] = other_ref[...]
    qt_ref[:, n:] = other_ref[...].T
    own.wait()
    qt_ref[:, :n] = q_ref[:n, :].T


def kernel(sizes, turn, split, *refs):
    n_x, n_y, n_z = sizes
    first, last = turn == 0, turn == len(TURNS) - 1
    side, begin, end = TURNS[turn]
    place_ref, d_ref, *refs = refs
    if first:
        given, ends_ref, refs = refs[:4], refs[4], refs[5:]
    else:
        q_ref, qt_ref, off_ref, w_ref, pos_ref, ends_ref, gq_in, found_in, *refs = refs
    piece = d_ref.shape[0] // (len(SIDES) * n_z)
    nd = (end - begin) * n_z * piece
    d_ref = d_ref.at[pl.ds(begin * n_z * piece, nd)]
    outs = nd // split
    gd_refs, refs = refs[:outs], refs[outs:]
    gq_ref, found_ref, *refs = refs
    if first:
        q_ref, qt_ref, off_ref, w_ref, pos_ref, *refs = refs
        lay_out(*given, q_ref, qt_ref, off_ref, w_ref, pos_ref, refs[-1].at[nd // SUB])
    nq = q_ref.shape[0]
    dt_ref, id_ref, c_ref, gd_ref, sems = refs

    if last:
        top = lax.broadcasted_iota(jnp.int32, found_ref.shape, 0) == 0
        found_ref[...] = jnp.where(top, ends_ref[...], 0.0)
    x, y, core = place_ref[0], place_ref[1], place_ref[2]
    row = lax.broadcasted_iota(jnp.int32, (piece, 128), 0)
    for step, across in enumerate(SIDES[begin:end]):
        from_x = (x - jnp.where(core == 0, side, across) + n_x) % n_x
        from_y = (y - jnp.where(core == 0, across, side) + n_y) % n_y
        for j in range(n_z):
            z = j % (n_z // 2) + core * (n_z // 2)
            owner = core if j < n_z // 2 else 1 - core
            base = ((z * 2 + from_x // 2) * 2 + owner) * 2 * n_y + from_y * 2 + from_x % 2
            at = (step * n_z + j) * piece
            id_ref[at : at + piece, :] = row + base * piece
    dt_ref[...] = d_ref[...].T

    def front(tile, slot):
        cols = pl.ds(pl.multiple_of(tile * QT, QT), QT)
        q_t = qt_ref[:, cols]
        off = off_ref[:, cols]
        w = w_ref[:, cols]
        pos = pos_ref[:, cols]
        found = jnp.zeros((8, QT), F32)
        for r in range(0, nd, SUB):
            scores = jnp.dot(d_ref[r : r + SUB, :], q_t, preferred_element_type=F32)
            probs = jnp.exp2(scores * (0.0625 * LOG2E) - off)
            hits = jnp.concatenate([id_ref[r : r + SUB, :]] * (QT // 128), 1) == pos
            c_ref[slot, r : r + SUB, :] = (probs - jnp.where(hits, w, 0.0)).astype(BF16)
            found = found + jnp.sum(jnp.where(hits, scores, 0.0).reshape(SUB // 8, 8, QT), 0)
        if not first:
            found = found_in[:, cols] + found
        if last:
            found = 0.0625 * w * found
            width = found_ref.shape[1]
            for c in range(0, QT, width):
                found_ref[...] -= found[:, c : c + width]
        else:
            found_ref[:, cols] = found

    def back(tile, slot, opening=False, closing=False):
        cols = pl.ds(pl.multiple_of(tile * QT, QT), QT)
        q = q_ref[cols, :]
        leave = []
        for r in range(0, nd, SUB):
            rows = slice(r, r + SUB)
            term = jnp.dot(c_ref[slot, rows, :], q, preferred_element_type=F32)
            gd_ref[rows, :] = term if opening else gd_ref[rows, :] + term
            if closing:
                out = gd_refs[r // split].at[pl.ds(r % split, SUB)]
                leave.append(pltpu.make_async_copy(gd_ref.at[rows], out, sems.at[r // SUB]))
                leave[-1].start()
        term = jnp.dot(dt_ref[...], c_ref[slot], preferred_element_type=F32)
        gq_ref[:, cols] = term if first else gq_in[:, cols] + term
        for copy in leave:
            copy.wait()

    tiles = nq // QT
    front(0, 0)
    front(1, 1)
    back(0, 0, opening=True)

    def pair(i, _):
        tile = 2 * i + 1
        front(tile + 1, 0)
        back(tile, 1)
        front(tile + 2, 1)
        back(tile + 1, 0)
        return 0

    lax.fori_loop(0, (tiles - 2) // 2, pair, 0)
    back(tiles - 1, 1, closing=True)


def fused(turn, split, place, docs, asked, ends, sums, sizes):
    first, last = turn == 0, turn == len(TURNS) - 1
    nq = asked[0].shape[0] * (2 if first else 1)
    width = docs.shape[1]
    _, begin, end = TURNS[turn]
    nd = docs.shape[0] // len(SIDES) * (end - begin)
    vmem = pl.BlockSpec(memory_space=pltpu.VMEM)
    hbm = pl.BlockSpec(memory_space=pltpu.HBM)
    operands = [place, docs, *asked, ends, *sums]
    outs = nd // split
    out_shape = [pltpu.HBM((split, width), F32)] * outs
    out_shape += [jax.ShapeDtypeStruct((width, nq), F32), jax.ShapeDtypeStruct((8, width if last else nq), F32)]
    if first:
        line = jax.ShapeDtypeStruct((1, nq), F32)
        out_shape += [jax.ShapeDtypeStruct((nq, width), BF16), jax.ShapeDtypeStruct((width, nq), BF16)]
        out_shape += [line, line, jax.ShapeDtypeStruct((1, nq), jnp.int32)]
    return pl.pallas_call(
        functools.partial(kernel, sizes, turn, split),
        in_specs=[pl.BlockSpec(memory_space=pltpu.SMEM), vmem, hbm if first else vmem] + [vmem] * (len(operands) - 3),
        out_specs=[hbm] * outs + [vmem] * (len(out_shape) - outs),
        out_shape=out_shape,
        scratch_shapes=[
            pltpu.VMEM((width, nd), BF16),
            pltpu.VMEM((nd, 128), jnp.int32),
            pltpu.VMEM((2, nd, QT), BF16),
            pltpu.VMEM((nd, width), F32),
            pltpu.SemaphoreType.DMA((nd // SUB + 1,)),
        ],
        input_output_aliases={} if first else {8: outs},
        compiler_params=pltpu.CompilerParams(vmem_limit_bytes=VMEM_LIMIT),
        cost_estimate=pl.CostEstimate(flops=6 * nq * nd * width, bytes_accessed=8 << 20, transcendentals=nq * nd),
        name="fused",
    )(*operands)


def all_sides(array, along):
    return {side: moved(array, along, side) for side in (0, 2, 1, -1)}


def on_device(queries, documents, log_norms, weights, positives):
    own, width = queries.shape
    piece = documents.shape[0]
    total_q = own * lax.axis_size(AXES)
    n_x, n_y, n_z = lax.axis_size(X), lax.axis_size(Y), lax.axis_size("z")
    place = jnp.stack([lax.axis_index(X), lax.axis_index(Y), lax.axis_index("core")]).astype(jnp.int32)
    core = lax.axis_index("core")

    rows = jnp.stack([log_norms, weights, positives.astype(F32)])
    others = other_core(queries), other_core(rows)
    asked = (pltpu.with_memory_space_constraint(queries, pltpu.HBM), others[0], rows, others[1])

    column = lax.all_to_all(jnp.broadcast_to(documents[None], (n_z, piece, width)), "z", 0, 0, tiled=True)
    low, high = column.reshape(2, n_z // 2 * piece, width)
    mine, others = jnp.where(core == 0, low, high), jnp.where(core == 0, high, low)
    part = jnp.concatenate([mine, other_core(others)])
    near = all_sides(part, False)
    docs = all_sides(jnp.concatenate([near[s] for s in SIDES]), True)

    nd = docs[0].shape[0]
    terms = {}
    ends = (weights * log_norms).reshape(-1, width).sum(0)[None]
    sums = ()
    for turn, (side, begin, end) in enumerate(TURNS):
        count = nd // len(SIDES) * (end - begin)
        outs = 2 if side == 2 else 1
        got = fused(turn, count // outs, place, docs[side], asked, ends, sums, (n_x, n_y, n_z))
        terms.setdefault(side, []).extend(got[:outs])
        sums = grad_q, lost = got[outs : outs + 2]
        asked = got[outs + 2 :] or asked

    n = nd // 2
    far_a = moved(terms[2][0], True, -1)
    far_b = moved(terms[2][1], True, 1)
    behind = moved(jnp.concatenate([terms[-1][0][:n], terms[-1][0][n:] + far_b]), True, 1)
    ahead_a = moved(terms[1][0] + far_a, True, -1)
    ahead_b = moved(jnp.concatenate([terms[1][1], lost]), True, -1)
    lost = lost + moved(lost, True, 1) + moved(lost, True, 2) + ahead_b[n:]
    total = terms[0][0] + jnp.concatenate([ahead_a, ahead_b[:n]]) + behind
    n = nd // 4
    part = sum(
        moved(jnp.concatenate([total[i * n : (i + 1) * n], lost]), False, -s) for i, s in enumerate(SIDES)
    )
    mine, given = part[: n // 2], part[n // 2 :]
    got = other_core(given)
    lost = given[n // 2 :] + got[n // 2 :]
    got = got[: n // 2]
    low, high = jnp.where(core == 0, mine, got), jnp.where(core == 0, got, mine)
    part = jnp.concatenate([low, high]).reshape(n_z, piece, width)
    part = jnp.concatenate([part, jnp.broadcast_to(lost[None], (n_z, 8, width))], 1)
    part = lax.all_to_all(part, "z", 0, 0, tiled=True)
    part = part.sum(0)
    grad_documents = (part[:piece] * 0.0625).astype(BF16)
    loss = jnp.sum(part[piece:]) / total_q

    other_grad = grad_q[:, own:]
    other_grad = other_core(other_grad)
    grad_queries = ((grad_q[:, :own] + other_grad).T * 0.0625).astype(BF16)
    return (grad_queries, grad_documents, loss)


def solution(mesh):
    torus = Mesh(mesh.devices.reshape(8, 2, 2, 4, 2), AXES)
    placed = (P(AXES, None), P(AXES, None), P(AXES), P(AXES), P(AXES))
    return jax.shard_map(
        on_device,
        mesh=torus,
        in_specs=placed,
        out_specs=(P(AXES, None), P(AXES, None), P()),
        check_vma=False,
    )
```

profile of v0, /device:TPU:1, one launch (start us, length us, event | category | flops | bytes accessed | tf_op | source)
XLA Modules:
  0.0 125.2 jit_solution(3910129851924562539)
XLA Ops:
  0.6 1.4 %broadcast_in_dim.6 = bf16[8,32,256]{2,1,0:T(8,128)(2,1)} broadcast(bf16[32,256]{1,0:T(8,128)(2,1)} %param.6), dimensions={1,2} | broadcast | bytes 147456 | tf_op jit(solution)/shard_map/broadcast_in_dim | solution.py:209
  2.0 9.0 %all-to-all-start = ((bf16[8,32,256]{2,1,0:T(8,128)(2,1)}), bf16[8,32,256]{2,1,0:T(8,128)(2,1)S(1)}, u32[]{:S(2)}, u32[]{:S(2)}) async-start(bf16[8,32,256]{2,1,0:T(8,128)(2,1)} %broadcast_in_dim.6), calls=%async_computation | async-start | bytes 262144 | tf_op jit(solution)/shard_map/all_to_all | solution.py:209
  11.0 7.8 %all-to-all-done = bf16[8,32,256]{2,1,0:T(8,128)(2,1)S(1)} async-done(((bf16[8,32,256]{2,1,0:T(8,128)(2,1)}), bf16[8,32,256]{2,1,0:T(8,128)(2,1)S(1)}, u32[]{:S(2)}, u32[]{:S(2)}) %all-to-all-start) | async-done | bytes 131104 | tf_op jit(solution)/shard_map/all_to_all | solution.py:209
  18.8 2.4 %collective-permute-start = (bf16[128,256]{1,0:T(8,128)(2,1)S(1)}, bf16[128,256]{1,0:T(8,128)(2,1)S(1)}, u32[]{:S(2)}, u32[]{:S(2)}) collective-permute-start(bf16[128,256]{1,0:T(8,128)(2,1)S(1)} %bitcast.20), channel_id=1, source_target_pairs={{0,8},{8,0},{1,9},{9,1},{2,10},{10,2},{3,11},{11,3},{4,12},{12,4},... | collective-permute-start | bytes 196616 | tf_op jit(solution)/shard_map/ppermute | solution.py:29
  21.2 0.1 collective-permute-start.5
  21.3 0.7 convert_element_type.12
  22.0 0.1 collective-permute-done
  22.1 1.3 %collective-permute-start.1 = (bf16[256,256]{1,0:T(8,128)(2,1)S(1)}, bf16[256,256]{1,0:T(8,128)(2,1)S(1)}, u32[]{:S(2)}, u32[]{:S(2)}) collective-permute-start(bf16[256,256]{1,0:T(8,128)(2,1)S(1)} %pad_maximum_fusion.8), channel_id=1, source_target_pairs={{0,2},{2,4},{4,6},{6,0},{8,9},{10,11},{12,13},{14,15},{1,3},{3,5},... | collective-permute-start | bytes 393224 | tf_op jit(solution)/shard_map/ppermute | solution.py:46
  23.4 1.5 %collective-permute-start.2 = (bf16[256,256]{1,0:T(8,128)(2,1)S(1)}, bf16[256,256]{1,0:T(8,128)(2,1)S(1)}, u32[]{:S(2)}, u32[]{:S(2)}) collective-permute-start(bf16[256,256]{1,0:T(8,128)(2,1)S(1)} %pad_maximum_fusion.8), channel_id=1, source_target_pairs={{0,6},{2,0},{4,2},{6,4},{8,25},{10,27},{12,29},{14,31},{1,7},{3,1}... | collective-permute-start | bytes 393224 | tf_op jit(solution)/shard_map/ppermute | solution.py:46
  24.8 1.5 %collective-permute-start.3 = (bf16[256,256]{1,0:T(8,128)(2,1)S(1)}, bf16[256,256]{1,0:T(8,128)(2,1)S(1)}, u32[]{:S(2)}, u32[]{:S(2)}) collective-permute-start(bf16[256,256]{1,0:T(8,128)(2,1)S(1)} %pad_maximum_fusion.8), channel_id=1, source_target_pairs={{0,4},{2,6},{4,0},{6,2},{8,24},{10,26},{12,28},{14,30},{1,5},{3,7}... | collective-permute-start | bytes 393224 | tf_op jit(solution)/shard_map/ppermute | solution.py:46
  26.4 1.1 collective-permute-done.1
  27.5 2.9 %collective-permute-done.3 = bf16[256,256]{1,0:T(8,128)(2,1)S(1)} collective-permute-done((bf16[256,256]{1,0:T(8,128)(2,1)S(1)}, bf16[256,256]{1,0:T(8,128)(2,1)S(1)}, u32[]{:S(2)}, u32[]{:S(2)}) %collective-permute-start.3) | collective-permute-done | bytes 131104 | tf_op jit(solution)/shard_map/ppermute | solution.py:46
  30.5 2.7 %collective-permute-start.8 = (bf16[1024,256]{1,0:T(8,128)(2,1)S(1)}, bf16[1024,256]{1,0:T(8,128)(2,1)}, u32[]{:S(2)}, u32[]{:S(2)}) collective-permute-start(bf16[1024,256]{1,0:T(8,128)(2,1)S(1)} %constant_dynamic-update-slice_fusion.refs_1_), channel_id=1, source_target_pairs={{0,16},{2,18},{4,20},{6,22},{8,12},{10,14},{12,8},{14,10},{1,17},{... | collective-permute-start | bytes 1572872 | tf_op jit(solution)/shard_map/ppermute | solution.py:46
  33.2 0.7 pad_maximum_fusion.9.refs_4_
  33.9 2.3 %collective-permute-start.6 = (f32[3,1024]{1,0:T(4,128)S(1)}, f32[3,1024]{1,0:T(4,128)S(1)}, u32[]{:S(2)}, u32[]{:S(2)}) collective-permute-start(f32[3,1024]{1,0:T(4,128)S(1)} %pad_maximum_fusion.9.refs_4_), channel_id=1, source_target_pairs={{0,8},{8,0},{1,9},{9,1},{2,10},{10,2},{3,11},{11,3},{4,12},{12,4},... | collective-permute-start | bytes 36872 | tf_op jit(solution)/shard_map/ppermute | solution.py:29
  36.2 0.7 mul.20
  37.0 1.8 %collective-permute-start.7 = (bf16[1024,256]{1,0:T(8,128)(2,1)S(1)}, bf16[1024,256]{1,0:T(8,128)(2,1)S(1)}, u32[]{:S(2)}, u32[]{:S(2)}) collective-permute-start(bf16[1024,256]{1,0:T(8,128)(2,1)S(1)} %constant_dynamic-update-slice_fusion.refs_1_), channel_id=1, source_target_pairs={{0,17},{2,19},{4,21},{6,23},{8,14},{10,8},{12,10},{14,12},{1,0},{3... | collective-permute-start | bytes 1572872 | tf_op jit(solution)/shard_map/ppermute | solution.py:46
  38.8 6.3 %fused.5 = (f32[1024,256]{1,0:T(8,128)}, f32[256,2048]{1,0:T(8,128)S(1)}, f32[8,2048]{1,0:T(8,128)S(1)}, bf16[2048,256]{1,0:T(8,128)(2,1)S(1)}, bf16[256,2048]{1...) custom-call(s32[3]{0:T(128)S(1)} %pad_add_fusion.refs_0_, ...), custom_call_target="tpu_custom_call" | custom-call | flops 3221225472 | bytes 8388608 | tf_op jit(solution)/shard_map/fused/pallas_call | solution.py:174
  45.0 5.8 %fused.6 = (f32[512,256]{1,0:T(8,128)}, f32[512,256]{1,0:T(8,128)}, f32[256,2048]{1,0:T(8,128)S(1)}, f32[8,2048]{1,0:T(8,128)S(1)}) custom-call(s32[3]{0:T(128)S(1)} %pad_add_fusion.refs_0_, bf16[1024,256]{1,0:T(8,128)(2,1)} %collective-permute-done.8.refs_1_, bf16[2048,256]{1,0:T(8,128)(2,1)S(1)} %get-tuple-element.24.refs_2_, ...), custom_call_target="tpu_custom_call", output_to_operand_aliasing={{2}: (8, {})} | custom-call | flops 3221225472 | bytes 8388608 | tf_op jit(solution)/shard_map/fused/pallas_call | solution.py:174
  51.0 0.2 collective-permute-start.4
  51.1 2.6 %collective-permute-start.10 = (f32[512,256]{1,0:T(8,128)}, f32[512,256]{1,0:T(8,128)S(1)}, u32[]{:S(2)}, u32[]{:S(2)}) collective-permute-start(f32[512,256]{1,0:T(8,128)} %get-tuple-element.40), channel_id=1, source_target_pairs={{0,17},{2,19},{4,21},{6,23},{8,14},{10,8},{12,10},{14,12},{1,0},{3... | collective-permute-start | bytes 1572872 | tf_op jit(solution)/shard_map/ppermute | solution.py:46
  53.7 5.3 %fused.7 = (f32[1024,256]{1,0:T(8,128)}, f32[256,2048]{1,0:T(8,128)S(1)}, f32[8,2048]{1,0:T(8,128)S(1)}) custom-call(s32[3]{0:T(128)S(1)} %pad_add_fusion.refs_0_, bf16[1024,256]{1,0:T(8,128)(2,1)S(1)} %collective-permute-done.7.refs_1_, bf16[2048,256]{1,0:T(8,128)(2,1)S(1)} %get-tuple-element.24.refs_2_, ...), custom_call_target="tpu_custom_call", output_to_operand_aliasing={{1}: (8, {})} | custom-call | flops 3221225472 | bytes 8388608 | tf_op jit(solution)/shard_map/fused/pallas_call | solution.py:174
  59.1 1.6 %collective-permute-done.13 = f32[512,256]{1,0:T(8,128)S(1)} collective-permute-done((f32[512,256]{1,0:T(8,128)}, f32[512,256]{1,0:T(8,128)S(1)}, u32[]{:S(2)}, u32[]{:S(2)}) %collective-permute-start.13) | collective-permute-done | bytes 524320 | tf_op jit(solution)/shard_map/ppermute | solution.py:46
  60.7 1.3 %fusion.7 = (f32[512,256]{1,0:T(8,128)S(1)}, f32[512,256]{1,0:T(8,128)S(1)}) fusion(f32[1024,256]{1,0:T(8,128)} %get-tuple-element.43, f32[512,256]{1,0:T(8,128)S(1)} %collective-permute-done.13), kind=kLoop, calls=%fused_computation.34 | loop fusion | flops 131072 | bytes 2621440 | tf_op jit(solution)/shard_map/slice | solution.py:231
  62.2 4.1 %collective-permute-done.4.refs_1_ = bf16[1024,256]{1,0:T(8,128)(2,1)S(1)} collective-permute-done((bf16[1024,256]{1,0:T(8,128)(2,1)S(1)}, bf16[1024,256]{1,0:T(8,128)(2,1)S(1)}, u32[]{:S(2)}, u32[]{:S(2)}) %collective-permute-start.4) | collective-permute-done | bytes 524320 | tf_op jit(solution)/shard_map/ppermute | solution.py:46
  66.3 3.5 %fused.8 = (f32[512,256]{1,0:T(8,128)}, f32[256,2048]{1,0:T(8,128)S(1)}, f32[8,2048]{1,0:T(8,128)S(1)}) custom-call(s32[3]{0:T(128)S(1)} %pad_add_fusion.refs_0_, bf16[1024,256]{1,0:T(8,128)(2,1)S(1)} %collective-permute-done.4.refs_1_, bf16[2048,256]{1,0:T(8,128)(2,1)S(1)} %get-tuple-element.24.refs_2_, ...), custom_call_target="tpu_custom_call", output_to_operand_aliasing={{1}: (8, {})} | custom-call | flops 1610612736 | bytes 8388608 | tf_op jit(solution)/shard_map/fused/pallas_call | solution.py:174
  69.9 3.6 %fused.9 = (f32[512,256]{1,0:T(8,128)}, f32[256,2048]{1,0:T(8,128)S(1)}, f32[8,256]{1,0:T(8,128)S(1)}) custom-call(s32[3]{0:T(128)S(1)} %pad_add_fusion.refs_0_, bf16[1024,256]{1,0:T(8,128)(2,1)S(1)} %collective-permute-done.4.refs_1_, bf16[2048,256]{1,0:T(8,128)(2,1)S(1)} %get-tuple-element.24.refs_2_, ...), custom_call_target="tpu_custom_call", output_to_operand_aliasing={{1}: (8, {})} | custom-call | flops 1610612736 | bytes 8388608 | tf_op jit(solution)/shard_map/fused/pallas_call | solution.py:174
  73.5 1.2 pad_maximum_fusion.5
  74.9 1.5 %collective-permute-start.15 = (f32[8,256]{1,0:T(8,128)S(1)}, f32[8,256]{1,0:T(8,128)S(1)}, u32[]{:S(2)}, u32[]{:S(2)}) collective-permute-start(f32[8,256]{1,0:T(8,128)S(1)} %get-tuple-element.42), channel_id=1, source_target_pairs={{0,1},{2,3},{4,5},{6,7},{8,10},{10,12},{12,14},{14,8},{1,16},{3,18... | collective-permute-start | bytes 24584 | tf_op jit(solution)/shard_map/ppermute | solution.py:46
  76.5 1.7 %collective-permute-start.16 = (f32[8,256]{1,0:T(8,128)S(1)}, f32[8,256]{1,0:T(8,128)S(1)}, u32[]{:S(2)}, u32[]{:S(2)}) collective-permute-start(f32[8,256]{1,0:T(8,128)S(1)} %get-tuple-element.42), channel_id=1, source_target_pairs={{0,16},{2,18},{4,20},{6,22},{8,12},{10,14},{12,8},{14,10},{1,17},{... | collective-permute-start | bytes 24584 | tf_op jit(solution)/shard_map/ppermute | solution.py:46
  78.2 5.0 %collective-permute-done.12 = f32[520,256]{1,0:T(8,128)S(1)} collective-permute-done((f32[520,256]{1,0:T(8,128)S(1)}, f32[520,256]{1,0:T(8,128)S(1)}, u32[]{:S(2)}, u32[]{:S(2)}) %collective-permute-start.12) | collective-permute-done | bytes 532512 | tf_op jit(solution)/shard_map/ppermute | solution.py:46
  83.2 5.5 %collective-permute-done.11 = f32[512,256]{1,0:T(8,128)S(1)} collective-permute-done((f32[512,256]{1,0:T(8,128)S(1)}, f32[512,256]{1,0:T(8,128)S(1)}, u32[]{:S(2)}, u32[]{:S(2)}) %collective-permute-start.11) | collective-permute-done | bytes 524320 | tf_op jit(solution)/shard_map/ppermute | solution.py:46
  88.8 0.2 fusion
  89.1 0.6 collective-permute-start.17
  89.8 0.9 collective-permute-start.18
  90.7 0.4 collective-permute-start.19
  91.1 3.8 %collective-permute-done.17 = f32[264,256]{1,0:T(8,128)S(1)} collective-permute-done((f32[264,256]{1,0:T(8,128)S(1)}, f32[264,256]{1,0:T(8,128)S(1)}, u32[]{:S(2)}, u32[]{:S(2)}) %collective-permute-start.17) | collective-permute-done | bytes 270368 | tf_op jit(solution)/shard_map/ppermute | solution.py:46
  94.8 4.7 %collective-permute-done.18 = f32[264,256]{1,0:T(8,128)S(1)} collective-permute-done((f32[264,256]{1,0:T(8,128)S(1)}, f32[264,256]{1,0:T(8,128)S(1)}, u32[]{:S(2)}, u32[]{:S(2)}) %collective-permute-start.18) | collective-permute-done | bytes 270368 | tf_op jit(solution)/shard_map/ppermute | solution.py:46
  99.5 0.1 fusion.4
  99.6 3.5 %collective-permute-start.20 = (f32[136,256]{1,0:T(8,128)S(1)}, f32[136,256]{1,0:T(8,128)S(1)}, u32[]{:S(2)}, u32[]{:S(2)}) collective-permute-start(f32[136,256]{1,0:T(8,128)S(1)} %slice.78), channel_id=1, source_target_pairs={{0,8},{8,0},{1,9},{9,1},{2,10},{10,2},{3,11},{11,3},{4,12},{12,4},... | collective-permute-start | bytes 417800 | tf_op jit(solution)/shard_map/ppermute | solution.py:29
  103.1 1.1 slice.55
  104.3 0.8 pad_maximum_fusion.6
  105.1 3.4 %all-to-all-start.1 = ((f32[8,40,256]{2,1,0:T(8,128)}), f32[8,40,256]{2,1,0:T(8,128)S(1)}, u32[]{:S(2)}, u32[]{:S(2)}) async-start(f32[8,40,256]{2,1,0:T(8,128)} %pad_maximum_fusion.6), calls=%async_computation.1 | async-start | bytes 655360 | tf_op jit(solution)/shard_map/all_to_all | solution.py:247
  108.5 1.4 %fusion.1 = bf16[1024,256]{0,1:T(8,128)(2,1)S(1)} fusion(f32[256,1024]{1,0:T(8,128)} %collective-permute-done.9, f32[256,2048]{1,0:T(8,128)S(1)} %get-tuple-element.37), kind=kLoop, calls=%fused_computation.9 | loop fusion | flops 786432 | bytes 2621440 | tf_op jit(solution)/shard_map/convert_element_type | solution.py:254
  110.0 1.0 copy.13
  111.0 11.2 %all-to-all-done.1 = f32[8,40,256]{2,1,0:T(8,128)S(1)} async-done(((f32[8,40,256]{2,1,0:T(8,128)}), f32[8,40,256]{2,1,0:T(8,128)S(1)}, u32[]{:S(2)}, u32[]{:S(2)}) %all-to-all-start.1) | async-done | bytes 327712 | tf_op jit(solution)/shard_map/all_to_all | solution.py:247
  122.2 0.6 fusion.5
  122.8 0.6 slice_reduce_fusion
  (43 shorter events, 1.0 us)
Async XLA Ops:
  2.0 16.8 %all-to-all-start = ((bf16[8,32,256]{2,1,0:T(8,128)(2,1)}), bf16[8,32,256]{2,1,0:T(8,128)(2,1)S(1)}, u32[]{:S(2)}, u32[]{:S(2)}) async-start(bf16[8,32,256]{2,1,0:T(8,128)(2,1)} %broadcast_in_dim.6), calls=%async_computation | async-start | bytes 262144 | tf_op jit(solution)/shard_map/all_to_all | solution.py:209
  18.8 3.3 %collective-permute-start = (bf16[128,256]{1,0:T(8,128)(2,1)S(1)}, bf16[128,256]{1,0:T(8,128)(2,1)S(1)}, u32[]{:S(2)}, u32[]{:S(2)}) collective-permute-start(bf16[128,256]{1,0:T(8,128)(2,1)S(1)} %bitcast.20), channel_id=1, source_target_pairs={{0,8},{8,0},{1,9},{9,1},{2,10},{10,2},{3,11},{11,3},{4,12},{12,4},... | collective-permute-start | bytes 196616 | tf_op jit(solution)/shard_map/ppermute | solution.py:29
  21.2 17.6 %collective-permute-start.5 = (bf16[1024,256]{1,0:T(8,128)(2,1)}, bf16[1024,256]{1,0:T(8,128)(2,1)S(1)}, u32[]{:S(2)}, u32[]{:S(2)}) collective-permute-start(bf16[1024,256]{1,0:T(8,128)(2,1)} %refs_2_.1), channel_id=1, source_target_pairs={{0,8},{8,0},{1,9},{9,1},{2,10},{10,2},{3,11},{11,3},{4,12},{12,4},... | collective-permute-start | bytes 1572872 | tf_op jit(solution)/shard_map/ppermute | solution.py:29
  22.1 5.4 %collective-permute-start.1 = (bf16[256,256]{1,0:T(8,128)(2,1)S(1)}, bf16[256,256]{1,0:T(8,128)(2,1)S(1)}, u32[]{:S(2)}, u32[]{:S(2)}) collective-permute-start(bf16[256,256]{1,0:T(8,128)(2,1)S(1)} %pad_maximum_fusion.8), channel_id=1, source_target_pairs={{0,2},{2,4},{4,6},{6,0},{8,9},{10,11},{12,13},{14,15},{1,3},{3,5},... | collective-permute-start | bytes 393224 | tf_op jit(solution)/shard_map/ppermute | solution.py:46
  23.4 4.1 %collective-permute-start.2 = (bf16[256,256]{1,0:T(8,128)(2,1)S(1)}, bf16[256,256]{1,0:T(8,128)(2,1)S(1)}, u32[]{:S(2)}, u32[]{:S(2)}) collective-permute-start(bf16[256,256]{1,0:T(8,128)(2,1)S(1)} %pad_maximum_fusion.8), channel_id=1, source_target_pairs={{0,6},{2,0},{4,2},{6,4},{8,25},{10,27},{12,29},{14,31},{1,7},{3,1}... | collective-permute-start | bytes 393224 | tf_op jit(solution)/shard_map/ppermute | solution.py:46
  24.8 5.6 %collective-permute-start.3 = (bf16[256,256]{1,0:T(8,128)(2,1)S(1)}, bf16[256,256]{1,0:T(8,128)(2,1)S(1)}, u32[]{:S(2)}, u32[]{:S(2)}) collective-permute-start(bf16[256,256]{1,0:T(8,128)(2,1)S(1)} %pad_maximum_fusion.8), channel_id=1, source_target_pairs={{0,4},{2,6},{4,0},{6,2},{8,24},{10,26},{12,28},{14,30},{1,5},{3,7}... | collective-permute-start | bytes 393224 | tf_op jit(solution)/shard_map/ppermute | solution.py:46
  30.5 14.6 %collective-permute-start.8 = (bf16[1024,256]{1,0:T(8,128)(2,1)S(1)}, bf16[1024,256]{1,0:T(8,128)(2,1)}, u32[]{:S(2)}, u32[]{:S(2)}) collective-permute-start(bf16[1024,256]{1,0:T(8,128)(2,1)S(1)} %constant_dynamic-update-slice_fusion.refs_1_), channel_id=1, source_target_pairs={{0,16},{2,18},{4,20},{6,22},{8,12},{10,14},{12,8},{14,10},{1,17},{... | collective-permute-start | bytes 1572872 | tf_op jit(solution)/shard_map/ppermute | solution.py:46
  33.9 4.8 %collective-permute-start.6 = (f32[3,1024]{1,0:T(4,128)S(1)}, f32[3,1024]{1,0:T(4,128)S(1)}, u32[]{:S(2)}, u32[]{:S(2)}) collective-permute-start(f32[3,1024]{1,0:T(4,128)S(1)} %pad_maximum_fusion.9.refs_4_), channel_id=1, source_target_pairs={{0,8},{8,0},{1,9},{9,1},{2,10},{10,2},{3,11},{11,3},{4,12},{12,4},... | collective-permute-start | bytes 36872 | tf_op jit(solution)/shard_map/ppermute | solution.py:29
  37.0 16.7 %collective-permute-start.7 = (bf16[1024,256]{1,0:T(8,128)(2,1)S(1)}, bf16[1024,256]{1,0:T(8,128)(2,1)S(1)}, u32[]{:S(2)}, u32[]{:S(2)}) collective-permute-start(bf16[1024,256]{1,0:T(8,128)(2,1)S(1)} %constant_dynamic-update-slice_fusion.refs_1_), channel_id=1, source_target_pairs={{0,17},{2,19},{4,21},{6,23},{8,14},{10,8},{12,10},{14,12},{1,0},{3... | collective-permute-start | bytes 1572872 | tf_op jit(solution)/shard_map/ppermute | solution.py:46
  50.9 9.8 %collective-permute-start.13 = (f32[512,256]{1,0:T(8,128)}, f32[512,256]{1,0:T(8,128)S(1)}, u32[]{:S(2)}, u32[]{:S(2)}) collective-permute-start(f32[512,256]{1,0:T(8,128)} %get-tuple-element.44), channel_id=1, source_target_pairs={{0,1},{2,3},{4,5},{6,7},{8,10},{10,12},{12,14},{14,8},{1,16},{3,18... | collective-permute-start | bytes 1572872 | tf_op jit(solution)/shard_map/ppermute | solution.py:46
  51.0 15.4 %collective-permute-start.4 = (bf16[1024,256]{1,0:T(8,128)(2,1)S(1)}, bf16[1024,256]{1,0:T(8,128)(2,1)S(1)}, u32[]{:S(2)}, u32[]{:S(2)}) collective-permute-start(bf16[1024,256]{1,0:T(8,128)(2,1)S(1)} %constant_dynamic-update-slice_fusion.refs_1_), channel_id=1, source_target_pairs={{0,1},{2,3},{4,5},{6,7},{8,10},{10,12},{12,14},{14,8},{1,16},{3,18... | collective-permute-start | bytes 1572872 | tf_op jit(solution)/shard_map/ppermute | solution.py:46
  51.1 23.6 %collective-permute-start.10 = (f32[512,256]{1,0:T(8,128)}, f32[512,256]{1,0:T(8,128)S(1)}, u32[]{:S(2)}, u32[]{:S(2)}) collective-permute-start(f32[512,256]{1,0:T(8,128)} %get-tuple-element.40), channel_id=1, source_target_pairs={{0,17},{2,19},{4,21},{6,23},{8,14},{10,8},{12,10},{14,12},{1,0},{3... | collective-permute-start | bytes 1572872 | tf_op jit(solution)/shard_map/ppermute | solution.py:46
  62.1 26.7 %collective-permute-start.14 = (f32[1024,256]{1,0:T(8,128)S(1)}, f32[1024,256]{1,0:T(8,128)S(1)}, u32[]{:S(2)}, u32[]{:S(2)}) collective-permute-start(f32[1024,256]{1,0:T(8,128)S(1)} %pad_maximum_fusion), channel_id=1, source_target_pairs={{0,1},{2,3},{4,5},{6,7},{8,10},{10,12},{12,14},{14,8},{1,16},{3,18... | collective-permute-start | bytes 3145736 | tf_op jit(solution)/shard_map/ppermute | solution.py:46
  69.9 4.9 %copy-start.1 = (f32[512,256]{1,0:T(8,128)S(1)}, f32[512,256]{1,0:T(8,128)}, u32[]{:S(2)}) copy-start(f32[512,256]{1,0:T(8,128)} %get-tuple-element.39) | copy-start | bytes 1572868
  73.5 15.3 %copy-start = (f32[1024,256]{1,0:T(8,128)S(1)}, f32[1024,256]{1,0:T(8,128)}, u32[]{:S(2)}) copy-start(f32[1024,256]{1,0:T(8,128)} %get-tuple-element.38) | copy-start | bytes 3145732
  74.7 8.5 %collective-permute-start.12 = (f32[520,256]{1,0:T(8,128)S(1)}, f32[520,256]{1,0:T(8,128)S(1)}, u32[]{:S(2)}, u32[]{:S(2)}) collective-permute-start(f32[520,256]{1,0:T(8,128)S(1)} %pad_maximum_fusion.5), channel_id=1, source_target_pairs={{0,17},{2,19},{4,21},{6,23},{8,14},{10,8},{12,10},{14,12},{1,0},{3... | collective-permute-start | bytes 1597448 | tf_op jit(solution)/shard_map/ppermute | solution.py:46
  74.9 13.9 %collective-permute-start.11 = (f32[512,256]{1,0:T(8,128)S(1)}, f32[512,256]{1,0:T(8,128)S(1)}, u32[]{:S(2)}, u32[]{:S(2)}) collective-permute-start(f32[512,256]{1,0:T(8,128)S(1)} %add.41), channel_id=1, source_target_pairs={{0,17},{2,19},{4,21},{6,23},{8,14},{10,8},{12,10},{14,12},{1,0},{3... | collective-permute-start | bytes 1572872 | tf_op jit(solution)/shard_map/ppermute | solution.py:46
  74.9 8.3 %collective-permute-start.15 = (f32[8,256]{1,0:T(8,128)S(1)}, f32[8,256]{1,0:T(8,128)S(1)}, u32[]{:S(2)}, u32[]{:S(2)}) collective-permute-start(f32[8,256]{1,0:T(8,128)S(1)} %get-tuple-element.42), channel_id=1, source_target_pairs={{0,1},{2,3},{4,5},{6,7},{8,10},{10,12},{12,14},{14,8},{1,16},{3,18... | collective-permute-start | bytes 24584 | tf_op jit(solution)/shard_map/ppermute | solution.py:46
  76.5 6.8 %collective-permute-start.16 = (f32[8,256]{1,0:T(8,128)S(1)}, f32[8,256]{1,0:T(8,128)S(1)}, u32[]{:S(2)}, u32[]{:S(2)}) collective-permute-start(f32[8,256]{1,0:T(8,128)S(1)} %get-tuple-element.42), channel_id=1, source_target_pairs={{0,16},{2,18},{4,20},{6,22},{8,12},{10,14},{12,8},{14,10},{1,17},{... | collective-permute-start | bytes 24584 | tf_op jit(solution)/shard_map/ppermute | solution.py:46
  89.1 5.7 %collective-permute-start.17 = (f32[264,256]{1,0:T(8,128)S(1)}, f32[264,256]{1,0:T(8,128)S(1)}, u32[]{:S(2)}, u32[]{:S(2)}) collective-permute-start(f32[264,256]{1,0:T(8,128)S(1)} %get-tuple-element.61), channel_id=1, source_target_pairs={{0,6},{2,0},{4,2},{6,4},{8,25},{10,27},{12,29},{14,31},{1,7},{3,1}... | collective-permute-start | bytes 811016 | tf_op jit(solution)/shard_map/ppermute | solution.py:46
  89.8 9.7 %collective-permute-start.18 = (f32[264,256]{1,0:T(8,128)S(1)}, f32[264,256]{1,0:T(8,128)S(1)}, u32[]{:S(2)}, u32[]{:S(2)}) collective-permute-start(f32[264,256]{1,0:T(8,128)S(1)} %get-tuple-element.62), channel_id=1, source_target_pairs={{0,2},{2,4},{4,6},{6,0},{8,9},{10,11},{12,13},{14,15},{1,3},{3,5},... | collective-permute-start | bytes 811016 | tf_op jit(solution)/shard_map/ppermute | solution.py:46
  90.7 8.8 %collective-permute-start.19 = (f32[264,256]{1,0:T(8,128)S(1)}, f32[264,256]{1,0:T(8,128)S(1)}, u32[]{:S(2)}, u32[]{:S(2)}) collective-permute-start(f32[264,256]{1,0:T(8,128)S(1)} %get-tuple-element.63), channel_id=1, source_target_pairs={{0,4},{2,6},{4,0},{6,2},{8,24},{10,26},{12,28},{14,30},{1,5},{3,7}... | collective-permute-start | bytes 811016 | tf_op jit(solution)/shard_map/ppermute | solution.py:46
  99.6 4.6 %collective-permute-start.20 = (f32[136,256]{1,0:T(8,128)S(1)}, f32[136,256]{1,0:T(8,128)S(1)}, u32[]{:S(2)}, u32[]{:S(2)}) collective-permute-start(f32[136,256]{1,0:T(8,128)S(1)} %slice.78), channel_id=1, source_target_pairs={{0,8},{8,0},{1,9},{9,1},{2,10},{10,2},{3,11},{11,3},{4,12},{12,4},... | collective-permute-start | bytes 417800 | tf_op jit(solution)/shard_map/ppermute | solution.py:29
  104.2 4.3 %collective-permute-start.9 = (f32[256,1024]{1,0:T(8,128)}, f32[256,1024]{1,0:T(8,128)}, u32[]{:S(2)}, u32[]{:S(2)}) collective-permute-start(f32[256,1024]{1,0:T(8,128)} %slice.55), channel_id=1, source_target_pairs={{0,8},{8,0},{1,9},{9,1},{2,10},{10,2},{3,11},{11,3},{4,12},{12,4},... | collective-permute-start | bytes 3145736 | tf_op jit(solution)/shard_map/ppermute | solution.py:29
  105.1 17.1 %all-to-all-start.1 = ((f32[8,40,256]{2,1,0:T(8,128)}), f32[8,40,256]{2,1,0:T(8,128)S(1)}, u32[]{:S(2)}, u32[]{:S(2)}) async-start(f32[8,40,256]{2,1,0:T(8,128)} %pad_maximum_fusion.6), calls=%async_computation.1 | async-start | bytes 655360 | tf_op jit(solution)/shard_map/all_to_all | solution.py:247
where the time goes:
time: 126 us; the launch traced here: 125 us
  waiting for transfers between devices  47.9 us (38%)
  starting transfers between devices  37.7 us (30%)
  Pallas kernels  24.6 us (20%)
  other arithmetic  8.68 us (7%)
  local copies, waits for them, and re-layouts  3.65 us (3%)
  between operations  2.7 us (2%)
    ppermute x16, waiting for transfers between devices, moved(): return lax.ppermute(array, CHIPS, route)  28.8 us
    pallas_call x5, Pallas kernels, fused(): pl.pallas_call(functools.partial(kernel, sizes, turn, split), in_specs=[p...  24.6 us
    ppermute x16, starting transfers between devices, moved(): return lax.ppermute(array, CHIPS, route)  17 us
    all_to_all x1, waiting for transfers between devices, on_device(): part = lax.all_to_all(part, 'z', 0, 0, tiled=True)  11.2 us
    all_to_all x1, starting transfers between devices, on_device(): lax.all_to_all(jnp.broadcast_to(documents[None], (n_z, piece, width)), 'z...  9 us
    ppermute x5, starting transfers between devices, other_core(): return lax.ppermute(array, 'core', [(0, 1), (1, 0)])  8.29 us
    all_to_all x1, waiting for transfers between devices, on_device(): lax.all_to_all(jnp.broadcast_to(documents[None], (n_z, piece, width)), 'z...  7.75 us
    all_to_all x1, starting transfers between devices, on_device(): part = lax.all_to_all(part, 'z', 0, 0, tiled=True)  3.43 us
  transfers between devices with their start and end apart: 23, of which 11 were waited for; matrix products, arithmetic and copies ran while one was open for 7% of the time, Pallas kernels for 20%

commit v1 on v0

--- a/solution.py
+++ b/solution.py
@@ -20,7 +20,7 @@
 LOG2E = math.log2(math.e)
 QT = 512
 SUB = 256
-SIDES = (0, 1, -1, 2)
+SIDES = (0, 2, 1, -1)
 TURNS = ((0, 0, 4), (2, 0, 4), (-1, 0, 4), (1, 0, 2), (1, 2, 4))
 VMEM_LIMIT = 16 << 20
 
@@ -135,6 +135,10 @@
                 leave[-1].start()
         term = jnp.dot(dt_ref[...], c_ref[slot], preferred_element_type=F32)
         gq_ref[:, cols] = term if first else gq_in[:, cols] + term
+        if closing and last:
+            out = gd_refs[-1].at[pl.ds(split, found_ref.shape[0])]
+            leave.append(pltpu.make_async_copy(found_ref, out, sems.at[nd // SUB]))
+            leave[-1].start()
         for copy in leave:
             copy.wait()
 
@@ -165,7 +169,7 @@
     hbm = pl.BlockSpec(memory_space=pltpu.HBM)
     operands = [place, docs, *asked, ends, *sums]
     outs = nd // split
-    out_shape = [pltpu.HBM((split, width), F32)] * outs
+    out_shape = [pltpu.HBM((split + 8 if last else split, width), F32)] * outs
     out_shape += [jax.ShapeDtypeStruct((width, nq), F32), jax.ShapeDtypeStruct((8, width if last else nq), F32)]
     if first:
         line = jax.ShapeDtypeStruct((1, nq), F32)
@@ -219,7 +223,7 @@
     sums = ()
     for turn, (side, begin, end) in enumerate(TURNS):
         count = nd // len(SIDES) * (end - begin)
-        outs = 2 if side == 2 else 1
+        outs = count * 2 // nd
         got = fused(turn, count // outs, place, docs[side], asked, ends, sums, (n_x, n_y, n_z))
         terms.setdefault(side, []).extend(got[:outs])
         sums = grad_q, lost = got[outs : outs + 2]
@@ -228,18 +232,22 @@
     n = nd // 2
     far_a = moved(terms[2][0], True, -1)
     far_b = moved(terms[2][1], True, 1)
-    behind = moved(jnp.concatenate([terms[-1][0][:n], terms[-1][0][n:] + far_b]), True, 1)
+    behind_a = moved(terms[-1][0], True, 1)
+    behind_b = moved(terms[-1][1] + far_b, True, 1)
     ahead_a = moved(terms[1][0] + far_a, True, -1)
-    ahead_b = moved(jnp.concatenate([terms[1][1], lost]), True, -1)
+    ahead_b = moved(terms[1][1], True, -1)
     lost = lost + moved(lost, True, 1) + moved(lost, True, 2) + ahead_b[n:]
-    total = terms[0][0] + jnp.concatenate([ahead_a, ahead_b[:n]]) + behind
+    near = terms[0][0] + ahead_a + behind_a
+    next_to = terms[0][1] + ahead_b[:n] + behind_b
     n = nd // 4
-    part = sum(
-        moved(jnp.concatenate([total[i * n : (i + 1) * n], lost]), False, -s) for i, s in enumerate(SIDES)
-    )
+    opposite = moved(near[n:], False, -2)
+    one = moved(jnp.concatenate([next_to[:n], lost]), False, -1)
+    other = moved(jnp.concatenate([next_to[n:], lost]), False, 1)
+    lost = lost + moved(lost, False, 2) + one[n:] + other[n:]
+    part = near[:n] + opposite + one[:n] + other[:n]
     mine, given = part[: n // 2], part[n // 2 :]
-    got = other_core(given)
-    lost = given[n // 2 :] + got[n // 2 :]
+    got = other_core(jnp.concatenate([given, lost]))
+    lost = lost + got[n // 2 :]
     got = got[: n // 2]
     low, high = jnp.where(core == 0, mine, got), jnp.where(core == 0, got, mine)
     part = jnp.concatenate([low, high]).reshape(n_z, piece, width)

time: 126 us -> 124 us (0.984)
  the two profiles are of different devices: /device:TPU:1 before, /device:TPU:7 now
where the time goes in v1:
time: 124 us
  starting transfers between devices  46.9 us (38%)
  waiting for transfers between devices  39.7 us (32%)
  Pallas kernels  24.6 us (20%)
  other arithmetic  6.24 us (5%)
  local copies, waits for them, and re-layouts  3.58 us (3%)
  between operations  2.72 us (2%)
    ppermute x18, starting transfers between devices, moved(): return lax.ppermute(array, CHIPS, route)  26.5 us
    pallas_call x5, Pallas kernels, fused(): pl.pallas_call(functools.partial(kernel, sizes, turn, split), in_specs=[p...  24.6 us
    ppermute x18, waiting for transfers between devices, moved(): return lax.ppermute(array, CHIPS, route)  20.7 us
    all_to_all x1, waiting for transfers between devices, on_device(): part = lax.all_to_all(part, 'z', 0, 0, tiled=True)  11.2 us
    ppermute x5, starting transfers between devices, other_core(): return lax.ppermute(array, 'core', [(0, 1), (1, 0)])  8.78 us
    all_to_all x1, starting transfers between devices, on_device(): lax.all_to_all(jnp.broadcast_to(documents[None], (n_z, piece, width)), 'z...  8.19 us
    all_to_all x1, waiting for transfers between devices, on_device(): lax.all_to_all(jnp.broadcast_to(documents[None], (n_z, piece, width)), 'z...  7.75 us
    all_to_all x1, starting transfers between devices, on_device(): part = lax.all_to_all(part, 'z', 0, 0, tiled=True)  3.43 us
  transfers between devices with their start and end apart: 25, of which 10 were waited for; matrix products, arithmetic and copies ran while one was open for 6% of the time, Pallas kernels for 20%

profile of v1, /device:TPU:7, one launch (start us, length us, event | category | flops | bytes accessed | tf_op | source)
XLA Modules:
  0.0 123.8 jit_solution(4392142595667891475)
XLA Ops:
  0.6 1.4 %broadcast_in_dim.6 = bf16[8,32,256]{2,1,0:T(8,128)(2,1)} broadcast(bf16[32,256]{1,0:T(8,128)(2,1)} %param.6), dimensions={1,2} | broadcast | bytes 147456 | tf_op jit(solution)/shard_map/broadcast_in_dim | solution.py:213
  2.0 8.2 %all-to-all-start = ((bf16[8,32,256]{2,1,0:T(8,128)(2,1)}), bf16[8,32,256]{2,1,0:T(8,128)(2,1)S(1)}, u32[]{:S(2)}, u32[]{:S(2)}) async-start(bf16[8,32,256]{2,1,0:T(8,128)(2,1)} %broadcast_in_dim.6), calls=%async_computation | async-start | bytes 262144 | tf_op jit(solution)/shard_map/all_to_all | solution.py:213
  10.2 7.8 %all-to-all-done = bf16[8,32,256]{2,1,0:T(8,128)(2,1)S(1)} async-done(((bf16[8,32,256]{2,1,0:T(8,128)(2,1)}), bf16[8,32,256]{2,1,0:T(8,128)(2,1)S(1)}, u32[]{:S(2)}, u32[]{:S(2)}) %all-to-all-start) | async-done | bytes 131104 | tf_op jit(solution)/shard_map/all_to_all | solution.py:213
  18.0 2.4 %collective-permute-start = (bf16[128,256]{1,0:T(8,128)(2,1)S(1)}, bf16[128,256]{1,0:T(8,128)(2,1)S(1)}, u32[]{:S(2)}, u32[]{:S(2)}) collective-permute-start(bf16[128,256]{1,0:T(8,128)(2,1)S(1)} %bitcast.20), channel_id=1, source_target_pairs={{0,8},{8,0},{1,9},{9,1},{2,10},{10,2},{3,11},{11,3},{4,12},{12,4},... | collective-permute-start | bytes 196616 | tf_op jit(solution)/shard_map/ppermute | solution.py:29
  20.4 0.1 collective-permute-start.5
  20.5 0.7 convert_element_type.12
  21.1 0.1 collective-permute-done
  21.3 1.2 collective-permute-start.1
  22.5 1.8 %collective-permute-start.2 = (bf16[256,256]{1,0:T(8,128)(2,1)S(1)}, bf16[256,256]{1,0:T(8,128)(2,1)S(1)}, u32[]{:S(2)}, u32[]{:S(2)}) collective-permute-start(bf16[256,256]{1,0:T(8,128)(2,1)S(1)} %pad_maximum_fusion.5), channel_id=1, source_target_pairs={{0,2},{2,4},{4,6},{6,0},{8,9},{10,11},{12,13},{14,15},{1,3},{3,5},... | collective-permute-start | bytes 393224 | tf_op jit(solution)/shard_map/ppermute | solution.py:46
  24.3 2.7 %collective-permute-done.1 = bf16[256,256]{1,0:T(8,128)(2,1)S(1)} collective-permute-done((bf16[256,256]{1,0:T(8,128)(2,1)S(1)}, bf16[256,256]{1,0:T(8,128)(2,1)S(1)}, u32[]{:S(2)}, u32[]{:S(2)}) %collective-permute-start.1) | collective-permute-done | bytes 131104 | tf_op jit(solution)/shard_map/ppermute | solution.py:46
  27.0 2.6 %collective-permute-done.3 = bf16[256,256]{1,0:T(8,128)(2,1)S(1)} collective-permute-done((bf16[256,256]{1,0:T(8,128)(2,1)S(1)}, bf16[256,256]{1,0:T(8,128)(2,1)S(1)}, u32[]{:S(2)}, u32[]{:S(2)}) %collective-permute-start.3) | collective-permute-done | bytes 131104 | tf_op jit(solution)/shard_map/ppermute | solution.py:46
  29.6 2.7 %collective-permute-start.8 = (bf16[1024,256]{1,0:T(8,128)(2,1)S(1)}, bf16[1024,256]{1,0:T(8,128)(2,1)}, u32[]{:S(2)}, u32[]{:S(2)}) collective-permute-start(bf16[1024,256]{1,0:T(8,128)(2,1)S(1)} %constant_dynamic-update-slice_fusion.refs_1_), channel_id=1, source_target_pairs={{0,16},{2,18},{4,20},{6,22},{8,12},{10,14},{12,8},{14,10},{1,17},{... | collective-permute-start | bytes 1572872 | tf_op jit(solution)/shard_map/ppermute | solution.py:46
  32.3 0.7 pad_maximum_fusion.6.refs_4_
  33.1 0.4 collective-permute-start.6
  33.5 0.7 mul.20
  34.2 3.0 %collective-permute-start.7 = (bf16[1024,256]{1,0:T(8,128)(2,1)S(1)}, bf16[1024,256]{1,0:T(8,128)(2,1)S(1)}, u32[]{:S(2)}, u32[]{:S(2)}) collective-permute-start(bf16[1024,256]{1,0:T(8,128)(2,1)S(1)} %constant_dynamic-update-slice_fusion.refs_1_), channel_id=1, source_target_pairs={{0,17},{2,19},{4,21},{6,23},{8,14},{10,8},{12,10},{14,12},{1,0},{3... | collective-permute-start | bytes 1572872 | tf_op jit(solution)/shard_map/ppermute | solution.py:46
  37.3 6.2 %fused.5 = (f32[512,256]{1,0:T(8,128)}, f32[512,256]{1,0:T(8,128)}, f32[256,2048]{1,0:T(8,128)S(1)}, f32[8,2048]{1,0:T(8,128)S(1)}, bf16[2048,256]{1,0:T(8,128)(...) custom-call(s32[3]{0:T(128)S(1)} %pad_add_fusion.refs_0_, ...), custom_call_target="tpu_custom_call" | custom-call | flops 3221225472 | bytes 8388608 | tf_op jit(solution)/shard_map/fused/pallas_call | solution.py:178
  43.5 5.8 %fused.6 = (f32[512,256]{1,0:T(8,128)}, f32[512,256]{1,0:T(8,128)}, f32[256,2048]{1,0:T(8,128)S(1)}, f32[8,2048]{1,0:T(8,128)S(1)}) custom-call(s32[3]{0:T(128)S(1)} %pad_add_fusion.refs_0_, bf16[1024,256]{1,0:T(8,128)(2,1)} %collective-permute-done.8.refs_1_, bf16[2048,256]{1,0:T(8,128)(2,1)S(1)} %get-tuple-element.26.refs_2_, ...), custom_call_target="tpu_custom_call", output_to_operand_aliasing={{2}: (8, {})} | custom-call | flops 3221225472 | bytes 8388608 | tf_op jit(solution)/shard_map/fused/pallas_call | solution.py:178
  49.3 0.3 collective-permute-start.15
  49.7 5.4 %fused.7 = (f32[512,256]{1,0:T(8,128)}, f32[512,256]{1,0:T(8,128)}, f32[256,2048]{1,0:T(8,128)S(1)}, f32[8,2048]{1,0:T(8,128)S(1)}) custom-call(s32[3]{0:T(128)S(1)} %pad_add_fusion.refs_0_, bf16[1024,256]{1,0:T(8,128)(2,1)S(1)} %collective-permute-done.7.refs_1_, bf16[2048,256]{1,0:T(8,128)(2,1)S(1)} %get-tuple-element.26.refs_2_, ...), custom_call_target="tpu_custom_call", output_to_operand_aliasing={{2}: (8, {})} | custom-call | flops 3221225472 | bytes 8388608 | tf_op jit(solution)/shard_map/fused/pallas_call | solution.py:178
  55.0 3.6 %fused.8 = (f32[512,256]{1,0:T(8,128)}, f32[256,2048]{1,0:T(8,128)S(1)}, f32[8,2048]{1,0:T(8,128)S(1)}) custom-call(s32[3]{0:T(128)S(1)} %pad_add_fusion.refs_0_, bf16[1024,256]{1,0:T(8,128)(2,1)S(1)} %collective-permute-done.4.refs_1_, bf16[2048,256]{1,0:T(8,128)(2,1)S(1)} %get-tuple-element.26.refs_2_, ...), custom_call_target="tpu_custom_call", output_to_operand_aliasing={{1}: (8, {})} | custom-call | flops 1610612736 | bytes 8388608 | tf_op jit(solution)/shard_map/fused/pallas_call | solution.py:178
  58.7 3.6 %fused.9 = (f32[520,256]{1,0:T(8,128)}, f32[256,2048]{1,0:T(8,128)S(1)}, f32[8,256]{1,0:T(8,128)S(1)}) custom-call(s32[3]{0:T(128)S(1)} %pad_add_fusion.refs_0_, bf16[1024,256]{1,0:T(8,128)(2,1)S(1)} %collective-permute-done.4.refs_1_, bf16[2048,256]{1,0:T(8,128)(2,1)S(1)} %get-tuple-element.26.refs_2_, ...), custom_call_target="tpu_custom_call", output_to_operand_aliasing={{1}: (8, {})} | custom-call | flops 1610612736 | bytes 8388608 | tf_op jit(solution)/shard_map/fused/pallas_call | solution.py:178
  62.3 2.7 %collective-permute-start.14 = (f32[520,256]{1,0:T(8,128)}, f32[520,256]{1,0:T(8,128)S(1)}, u32[]{:S(2)}, u32[]{:S(2)}) collective-permute-start(f32[520,256]{1,0:T(8,128)} %get-tuple-element.45), channel_id=1, source_target_pairs={{0,17},{2,19},{4,21},{6,23},{8,14},{10,8},{12,10},{14,12},{1,0},{3... | collective-permute-start | bytes 1597448 | tf_op jit(solution)/shard_map/ppermute | solution.py:46
  65.0 1.4 %collective-permute-start.10 = (f32[512,256]{1,0:T(8,128)S(1)}, f32[512,256]{1,0:T(8,128)S(1)}, u32[]{:S(2)}, u32[]{:S(2)}) collective-permute-start(f32[512,256]{1,0:T(8,128)S(1)} %copy-done.5), channel_id=1, source_target_pairs={{0,17},{2,19},{4,21},{6,23},{8,14},{10,8},{12,10},{14,12},{1,0},{3... | collective-permute-start | bytes 1572872 | tf_op jit(solution)/shard_map/ppermute | solution.py:46
  66.5 0.1 collective-permute-start.16
  66.7 0.1 collective-permute-start.17
  66.7 3.7 %collective-permute-start.18 = (f32[8,256]{1,0:T(8,128)S(1)}, f32[8,256]{1,0:T(8,128)S(1)}, u32[]{:S(2)}, u32[]{:S(2)}) collective-permute-start(f32[8,256]{1,0:T(8,128)S(1)} %get-tuple-element.48), channel_id=1, source_target_pairs={{0,16},{2,18},{4,20},{6,22},{8,12},{10,14},{12,8},{14,10},{1,17},{... | collective-permute-start | bytes 24584 | tf_op jit(solution)/shard_map/ppermute | solution.py:46
  70.5 6.7 %collective-permute-done.10 = f32[512,256]{1,0:T(8,128)S(1)} collective-permute-done((f32[512,256]{1,0:T(8,128)S(1)}, f32[512,256]{1,0:T(8,128)S(1)}, u32[]{:S(2)}, u32[]{:S(2)}) %collective-permute-start.10) | collective-permute-done | bytes 524320 | tf_op jit(solution)/shard_map/ppermute | solution.py:46
  77.2 1.5 %collective-permute-start.12 = (f32[512,256]{1,0:T(8,128)S(1)}, f32[512,256]{1,0:T(8,128)S(1)}, u32[]{:S(2)}, u32[]{:S(2)}) collective-permute-start(f32[512,256]{1,0:T(8,128)S(1)} %copy-done.4), channel_id=1, source_target_pairs={{0,1},{2,3},{4,5},{6,7},{8,10},{10,12},{12,14},{14,8},{1,16},{3,18... | collective-permute-start | bytes 1572872 | tf_op jit(solution)/shard_map/ppermute | solution.py:46
  78.7 2.0 %collective-permute-start.11 = (f32[512,256]{1,0:T(8,128)S(1)}, f32[512,256]{1,0:T(8,128)S(1)}, u32[]{:S(2)}, u32[]{:S(2)}) collective-permute-start(f32[512,256]{1,0:T(8,128)S(1)} %add.56), channel_id=1, source_target_pairs={{0,17},{2,19},{4,21},{6,23},{8,14},{10,8},{12,10},{14,12},{1,0},{3... | collective-permute-start | bytes 1572872 | tf_op jit(solution)/shard_map/ppermute | solution.py:46
  80.8 0.1 fusion.1
  81.1 2.7 %collective-permute-start.20 = (f32[264,256]{1,0:T(8,128)S(1)}, f32[264,256]{1,0:T(8,128)S(1)}, u32[]{:S(2)}, u32[]{:S(2)}) collective-permute-start(f32[264,256]{1,0:T(8,128)S(1)} %get-tuple-element.62), channel_id=1, source_target_pairs={{0,2},{2,4},{4,6},{6,0},{8,9},{10,11},{12,13},{14,15},{1,3},{3,5},... | collective-permute-start | bytes 811016 | tf_op jit(solution)/shard_map/ppermute | solution.py:46
  83.7 3.7 %collective-permute-done.12 = f32[512,256]{1,0:T(8,128)S(1)} collective-permute-done((f32[512,256]{1,0:T(8,128)S(1)}, f32[512,256]{1,0:T(8,128)S(1)}, u32[]{:S(2)}, u32[]{:S(2)}) %collective-permute-start.12) | collective-permute-done | bytes 524320 | tf_op jit(solution)/shard_map/ppermute | solution.py:46
  87.4 1.2 collective-permute-done.11
  88.7 0.1 add_add_fusion
  88.8 3.0 %collective-permute-start.13 = (f32[256,256]{1,0:T(8,128)S(1)}, f32[256,256]{1,0:T(8,128)S(1)}, u32[]{:S(2)}, u32[]{:S(2)}) collective-permute-start(f32[256,256]{1,0:T(8,128)S(1)} %slice.75), channel_id=1, source_target_pairs={{0,4},{2,6},{4,0},{6,2},{8,24},{10,26},{12,28},{14,30},{1,5},{3,7}... | collective-permute-start | bytes 786440 | tf_op jit(solution)/shard_map/ppermute | solution.py:46
  91.8 0.1 collective-permute-start.21
  91.9 3.7 %collective-permute-done.13 = f32[256,256]{1,0:T(8,128)S(1)} collective-permute-done((f32[256,256]{1,0:T(8,128)S(1)}, f32[256,256]{1,0:T(8,128)S(1)}, u32[]{:S(2)}, u32[]{:S(2)}) %collective-permute-start.13) | collective-permute-done | bytes 262176 | tf_op jit(solution)/shard_map/ppermute | solution.py:46
  95.6 0.1 slice_add_fusion.1
  95.8 5.9 %collective-permute-start.22 = (f32[136,256]{1,0:T(8,128)S(1)}, f32[136,256]{1,0:T(8,128)S(1)}, u32[]{:S(2)}, u32[]{:S(2)}) collective-permute-start(f32[136,256]{1,0:T(8,128)S(1)} %pad_maximum_fusion.4), channel_id=1, source_target_pairs={{0,8},{8,0},{1,9},{9,1},{2,10},{10,2},{3,11},{11,3},{4,12},{12,4},... | collective-permute-start | bytes 417800 | tf_op jit(solution)/shard_map/ppermute | solution.py:29
  101.8 1.0 slice.57
  102.9 0.8 pad_maximum_fusion.2
  103.7 3.4 %all-to-all-start.1 = ((f32[8,40,256]{2,1,0:T(8,128)}), f32[8,40,256]{2,1,0:T(8,128)S(1)}, u32[]{:S(2)}, u32[]{:S(2)}) async-start(f32[8,40,256]{2,1,0:T(8,128)} %pad_maximum_fusion.2), calls=%async_computation.1 | async-start | bytes 655360 | tf_op jit(solution)/shard_map/all_to_all | solution.py:255
  107.1 1.4 %fusion = bf16[1024,256]{0,1:T(8,128)(2,1)S(1)} fusion(f32[256,1024]{1,0:T(8,128)} %collective-permute-done.9, f32[256,2048]{1,0:T(8,128)S(1)} %get-tuple-element.39), kind=kLoop, calls=%fused_computation.1 | loop fusion | flops 786432 | bytes 2621440 | tf_op jit(solution)/shard_map/convert_element_type | solution.py:262
  108.6 1.0 copy.13
  109.6 11.2 %all-to-all-done.1 = f32[8,40,256]{2,1,0:T(8,128)S(1)} async-done(((f32[8,40,256]{2,1,0:T(8,128)}), f32[8,40,256]{2,1,0:T(8,128)S(1)}, u32[]{:S(2)}, u32[]{:S(2)}) %all-to-all-start.1) | async-done | bytes 327712 | tf_op jit(solution)/shard_map/all_to_all | solution.py:255
  120.8 0.6 fusion.2
  121.4 0.6 slice_reduce_fusion
  (56 shorter events, 0.8 us)
Async XLA Ops:
  2.0 15.9 %all-to-all-start = ((bf16[8,32,256]{2,1,0:T(8,128)(2,1)}), bf16[8,32,256]{2,1,0:T(8,128)(2,1)S(1)}, u32[]{:S(2)}, u32[]{:S(2)}) async-start(bf16[8,32,256]{2,1,0:T(8,128)(2,1)} %broadcast_in_dim.6), calls=%async_computation | async-start | bytes 262144 | tf_op jit(solution)/shard_map/all_to_all | solution.py:213
  18.0 3.3 %collective-permute-start = (bf16[128,256]{1,0:T(8,128)(2,1)S(1)}, bf16[128,256]{1,0:T(8,128)(2,1)S(1)}, u32[]{:S(2)}, u32[]{:S(2)}) collective-permute-start(bf16[128,256]{1,0:T(8,128)(2,1)S(1)} %bitcast.20), channel_id=1, source_target_pairs={{0,8},{8,0},{1,9},{9,1},{2,10},{10,2},{3,11},{11,3},{4,12},{12,4},... | collective-permute-start | bytes 196616 | tf_op jit(solution)/shard_map/ppermute | solution.py:29
  20.4 16.9 %collective-permute-start.5 = (bf16[1024,256]{1,0:T(8,128)(2,1)}, bf16[1024,256]{1,0:T(8,128)(2,1)S(1)}, u32[]{:S(2)}, u32[]{:S(2)}) collective-permute-start(bf16[1024,256]{1,0:T(8,128)(2,1)} %refs_2_.1), channel_id=1, source_target_pairs={{0,8},{8,0},{1,9},{9,1},{2,10},{10,2},{3,11},{11,3},{4,12},{12,4},... | collective-permute-start | bytes 1572872 | tf_op jit(solution)/shard_map/ppermute | solution.py:29
  21.3 5.7 %collective-permute-start.1 = (bf16[256,256]{1,0:T(8,128)(2,1)S(1)}, bf16[256,256]{1,0:T(8,128)(2,1)S(1)}, u32[]{:S(2)}, u32[]{:S(2)}) collective-permute-start(bf16[256,256]{1,0:T(8,128)(2,1)S(1)} %pad_maximum_fusion.5), channel_id=1, source_target_pairs={{0,4},{2,6},{4,0},{6,2},{8,24},{10,26},{12,28},{14,30},{1,5},{3,7}... | collective-permute-start | bytes 393224 | tf_op jit(solution)/shard_map/ppermute | solution.py:46
  22.5 4.5 %collective-permute-start.2 = (bf16[256,256]{1,0:T(8,128)(2,1)S(1)}, bf16[256,256]{1,0:T(8,128)(2,1)S(1)}, u32[]{:S(2)}, u32[]{:S(2)}) collective-permute-start(bf16[256,256]{1,0:T(8,128)(2,1)S(1)} %pad_maximum_fusion.5), channel_id=1, source_target_pairs={{0,2},{2,4},{4,6},{6,0},{8,9},{10,11},{12,13},{14,15},{1,3},{3,5},... | collective-permute-start | bytes 393224 | tf_op jit(solution)/shard_map/ppermute | solution.py:46
  24.3 5.3 %collective-permute-start.3 = (bf16[256,256]{1,0:T(8,128)(2,1)S(1)}, bf16[256,256]{1,0:T(8,128)(2,1)S(1)}, u32[]{:S(2)}, u32[]{:S(2)}) collective-permute-start(bf16[256,256]{1,0:T(8,128)(2,1)S(1)} %pad_maximum_fusion.5), channel_id=1, source_target_pairs={{0,6},{2,0},{4,2},{6,4},{8,25},{10,27},{12,29},{14,31},{1,7},{3,1}... | collective-permute-start | bytes 393224 | tf_op jit(solution)/shard_map/ppermute | solution.py:46
  29.6 13.9 %collective-permute-start.8 = (bf16[1024,256]{1,0:T(8,128)(2,1)S(1)}, bf16[1024,256]{1,0:T(8,128)(2,1)}, u32[]{:S(2)}, u32[]{:S(2)}) collective-permute-start(bf16[1024,256]{1,0:T(8,128)(2,1)S(1)} %constant_dynamic-update-slice_fusion.refs_1_), channel_id=1, source_target_pairs={{0,16},{2,18},{4,20},{6,22},{8,12},{10,14},{12,8},{14,10},{1,17},{... | collective-permute-start | bytes 1572872 | tf_op jit(solution)/shard_map/ppermute | solution.py:46
  33.1 4.2 %collective-permute-start.6 = (f32[3,1024]{1,0:T(4,128)S(1)}, f32[3,1024]{1,0:T(4,128)S(1)}, u32[]{:S(2)}, u32[]{:S(2)}) collective-permute-start(f32[3,1024]{1,0:T(4,128)S(1)} %pad_maximum_fusion.6.refs_4_), channel_id=1, source_target_pairs={{0,8},{8,0},{1,9},{9,1},{2,10},{10,2},{3,11},{11,3},{4,12},{12,4},... | collective-permute-start | bytes 36872 | tf_op jit(solution)/shard_map/ppermute | solution.py:29
  34.2 15.4 %collective-permute-start.7 = (bf16[1024,256]{1,0:T(8,128)(2,1)S(1)}, bf16[1024,256]{1,0:T(8,128)(2,1)S(1)}, u32[]{:S(2)}, u32[]{:S(2)}) collective-permute-start(bf16[1024,256]{1,0:T(8,128)(2,1)S(1)} %constant_dynamic-update-slice_fusion.refs_1_), channel_id=1, source_target_pairs={{0,17},{2,19},{4,21},{6,23},{8,14},{10,8},{12,10},{14,12},{1,0},{3... | collective-permute-start | bytes 1572872 | tf_op jit(solution)/shard_map/ppermute | solution.py:46
  37.2 17.8 %collective-permute-start.4 = (bf16[1024,256]{1,0:T(8,128)(2,1)S(1)}, bf16[1024,256]{1,0:T(8,128)(2,1)S(1)}, u32[]{:S(2)}, u32[]{:S(2)}) collective-permute-start(bf16[1024,256]{1,0:T(8,128)(2,1)S(1)} %constant_dynamic-update-slice_fusion.refs_1_), channel_id=1, source_target_pairs={{0,1},{2,3},{4,5},{6,7},{8,10},{10,12},{12,14},{14,8},{1,16},{3,18... | collective-permute-start | bytes 1572872 | tf_op jit(solution)/shard_map/ppermute | solution.py:46
  49.3 17.1 %collective-permute-start.15 = (f32[512,256]{1,0:T(8,128)}, f32[512,256]{1,0:T(8,128)S(1)}, u32[]{:S(2)}, u32[]{:S(2)}) collective-permute-start(f32[512,256]{1,0:T(8,128)} %get-tuple-element.47), channel_id=1, source_target_pairs={{0,1},{2,3},{4,5},{6,7},{8,10},{10,12},{12,14},{14,8},{1,16},{3,18... | collective-permute-start | bytes 1572872 | tf_op jit(solution)/shard_map/ppermute | solution.py:46
  58.6 6.4 %copy-start.5 = (f32[512,256]{1,0:T(8,128)S(1)}, f32[512,256]{1,0:T(8,128)}, u32[]{:S(2)}) copy-start(f32[512,256]{1,0:T(8,128)} %get-tuple-element.42) | copy-start | bytes 1572868
  58.6 7.8 %copy-start.1 = (f32[512,256]{1,0:T(8,128)S(1)}, f32[512,256]{1,0:T(8,128)}, u32[]{:S(2)}) copy-start(f32[512,256]{1,0:T(8,128)} %get-tuple-element.46) | copy-start | bytes 1572868
  58.6 18.5 %copy-start.4 = (f32[512,256]{1,0:T(8,128)S(1)}, f32[512,256]{1,0:T(8,128)}, u32[]{:S(2)}) copy-start(f32[512,256]{1,0:T(8,128)} %get-tuple-element.43) | copy-start | bytes 1572868
  58.6 20.0 %copy-start = (f32[512,256]{1,0:T(8,128)S(1)}, f32[512,256]{1,0:T(8,128)}, u32[]{:S(2)}) copy-start(f32[512,256]{1,0:T(8,128)} %get-tuple-element.41) | copy-start | bytes 1572868
  62.3 18.5 %copy-start.3 = (f32[512,256]{1,0:T(8,128)S(1)}, f32[512,256]{1,0:T(8,128)}, u32[]{:S(2)}) copy-start(f32[512,256]{1,0:T(8,128)} %get-tuple-element.44) | copy-start | bytes 1572868
  62.3 18.5 %collective-permute-start.14 = (f32[520,256]{1,0:T(8,128)}, f32[520,256]{1,0:T(8,128)S(1)}, u32[]{:S(2)}, u32[]{:S(2)}) collective-permute-start(f32[520,256]{1,0:T(8,128)} %get-tuple-element.45), channel_id=1, source_target_pairs={{0,17},{2,19},{4,21},{6,23},{8,14},{10,8},{12,10},{14,12},{1,0},{3... | collective-permute-start | bytes 1597448 | tf_op jit(solution)/shard_map/ppermute | solution.py:46
  65.0 12.1 %collective-permute-start.10 = (f32[512,256]{1,0:T(8,128)S(1)}, f32[512,256]{1,0:T(8,128)S(1)}, u32[]{:S(2)}, u32[]{:S(2)}) collective-permute-start(f32[512,256]{1,0:T(8,128)S(1)} %copy-done.5), channel_id=1, source_target_pairs={{0,17},{2,19},{4,21},{6,23},{8,14},{10,8},{12,10},{14,12},{1,0},{3... | collective-permute-start | bytes 1572872 | tf_op jit(solution)/shard_map/ppermute | solution.py:46
  66.5 14.2 %collective-permute-start.16 = (f32[512,256]{1,0:T(8,128)S(1)}, f32[512,256]{1,0:T(8,128)S(1)}, u32[]{:S(2)}, u32[]{:S(2)}) collective-permute-start(f32[512,256]{1,0:T(8,128)S(1)} %add.61), channel_id=1, source_target_pairs={{0,1},{2,3},{4,5},{6,7},{8,10},{10,12},{12,14},{14,8},{1,16},{3,18... | collective-permute-start | bytes 1572872 | tf_op jit(solution)/shard_map/ppermute | solution.py:46
  66.7 12.1 %collective-permute-start.17 = (f32[8,256]{1,0:T(8,128)S(1)}, f32[8,256]{1,0:T(8,128)S(1)}, u32[]{:S(2)}, u32[]{:S(2)}) collective-permute-start(f32[8,256]{1,0:T(8,128)S(1)} %get-tuple-element.48), channel_id=1, source_target_pairs={{0,1},{2,3},{4,5},{6,7},{8,10},{10,12},{12,14},{14,8},{1,16},{3,18... | collective-permute-start | bytes 24584 | tf_op jit(solution)/shard_map/ppermute | solution.py:46
  66.7 14.0 %collective-permute-start.18 = (f32[8,256]{1,0:T(8,128)S(1)}, f32[8,256]{1,0:T(8,128)S(1)}, u32[]{:S(2)}, u32[]{:S(2)}) collective-permute-start(f32[8,256]{1,0:T(8,128)S(1)} %get-tuple-element.48), channel_id=1, source_target_pairs={{0,16},{2,18},{4,20},{6,22},{8,12},{10,14},{12,8},{14,10},{1,17},{... | collective-permute-start | bytes 24584 | tf_op jit(solution)/shard_map/ppermute | solution.py:46
  77.2 10.3 %collective-permute-start.12 = (f32[512,256]{1,0:T(8,128)S(1)}, f32[512,256]{1,0:T(8,128)S(1)}, u32[]{:S(2)}, u32[]{:S(2)}) collective-permute-start(f32[512,256]{1,0:T(8,128)S(1)} %copy-done.4), channel_id=1, source_target_pairs={{0,1},{2,3},{4,5},{6,7},{8,10},{10,12},{12,14},{14,8},{1,16},{3,18... | collective-permute-start | bytes 1572872 | tf_op jit(solution)/shard_map/ppermute | solution.py:46
  78.7 9.9 %collective-permute-start.11 = (f32[512,256]{1,0:T(8,128)S(1)}, f32[512,256]{1,0:T(8,128)S(1)}, u32[]{:S(2)}, u32[]{:S(2)}) collective-permute-start(f32[512,256]{1,0:T(8,128)S(1)} %add.56), channel_id=1, source_target_pairs={{0,17},{2,19},{4,21},{6,23},{8,14},{10,8},{12,10},{14,12},{1,0},{3... | collective-permute-start | bytes 1572872 | tf_op jit(solution)/shard_map/ppermute | solution.py:46
  80.8 7.9 %copy-start.2 = (f32[512,256]{1,0:T(8,128)S(1)}, f32[512,256]{1,0:T(8,128)}, u32[]{:S(2)}) copy-start(f32[512,256]{1,0:T(8,128)} %get-tuple-element.40) | copy-start | bytes 1572868
  81.0 14.6 %collective-permute-start.19 = (f32[264,256]{1,0:T(8,128)S(1)}, f32[264,256]{1,0:T(8,128)S(1)}, u32[]{:S(2)}, u32[]{:S(2)}) collective-permute-start(f32[264,256]{1,0:T(8,128)S(1)} %get-tuple-element.61), channel_id=1, source_target_pairs={{0,6},{2,0},{4,2},{6,4},{8,25},{10,27},{12,29},{14,31},{1,7},{3,1}... | collective-permute-start | bytes 811016 | tf_op jit(solution)/shard_map/ppermute | solution.py:46
  81.1 14.6 %collective-permute-start.20 = (f32[264,256]{1,0:T(8,128)S(1)}, f32[264,256]{1,0:T(8,128)S(1)}, u32[]{:S(2)}, u32[]{:S(2)}) collective-permute-start(f32[264,256]{1,0:T(8,128)S(1)} %get-tuple-element.62), channel_id=1, source_target_pairs={{0,2},{2,4},{4,6},{6,0},{8,9},{10,11},{12,13},{14,15},{1,3},{3,5},... | collective-permute-start | bytes 811016 | tf_op jit(solution)/shard_map/ppermute | solution.py:46
  88.8 6.8 %collective-permute-start.13 = (f32[256,256]{1,0:T(8,128)S(1)}, f32[256,256]{1,0:T(8,128)S(1)}, u32[]{:S(2)}, u32[]{:S(2)}) collective-permute-start(f32[256,256]{1,0:T(8,128)S(1)} %slice.75), channel_id=1, source_target_pairs={{0,4},{2,6},{4,0},{6,2},{8,24},{10,26},{12,28},{14,30},{1,5},{3,7}... | collective-permute-start | bytes 786440 | tf_op jit(solution)/shard_map/ppermute | solution.py:46
  91.8 4.0 %collective-permute-start.21 = (f32[8,256]{1,0:T(8,128)S(1)}, f32[8,256]{1,0:T(8,128)S(1)}, u32[]{:S(2)}, u32[]{:S(2)}) collective-permute-start(f32[8,256]{1,0:T(8,128)S(1)} %slice_add_fusion.7), channel_id=1, source_target_pairs={{0,4},{2,6},{4,0},{6,2},{8,24},{10,26},{12,28},{14,30},{1,5},{3,7}... | collective-permute-start | bytes 24584 | tf_op jit(solution)/shard_map/ppermute | solution.py:46
  95.8 7.0 %collective-permute-start.22 = (f32[136,256]{1,0:T(8,128)S(1)}, f32[136,256]{1,0:T(8,128)S(1)}, u32[]{:S(2)}, u32[]{:S(2)}) collective-permute-start(f32[136,256]{1,0:T(8,128)S(1)} %pad_maximum_fusion.4), channel_id=1, source_target_pairs={{0,8},{8,0},{1,9},{9,1},{2,10},{10,2},{3,11},{11,3},{4,12},{12,4},... | collective-permute-start | bytes 417800 | tf_op jit(solution)/shard_map/ppermute | solution.py:29
  102.8 4.3 %collective-permute-start.9 = (f32[256,1024]{1,0:T(8,128)}, f32[256,1024]{1,0:T(8,128)}, u32[]{:S(2)}, u32[]{:S(2)}) collective-permute-start(f32[256,1024]{1,0:T(8,128)} %slice.57), channel_id=1, source_target_pairs={{0,8},{8,0},{1,9},{9,1},{2,10},{10,2},{3,11},{11,3},{4,12},{12,4},... | collective-permute-start | bytes 3145736 | tf_op jit(solution)/shard_map/ppermute | solution.py:29
  103.7 17.1 %all-to-all-start.1 = ((f32[8,40,256]{2,1,0:T(8,128)}), f32[8,40,256]{2,1,0:T(8,128)S(1)}, u32[]{:S(2)}, u32[]{:S(2)}) async-start(f32[8,40,256]{2,1,0:T(8,128)} %pad_maximum_fusion.2), calls=%async_computation.1 | async-start | bytes 655360 | tf_op jit(solution)/shard_map/all_to_all | solution.py:255

commit v2 on v0

--- a/solution.py
+++ b/solution.py
@@ -135,6 +135,10 @@
                 leave[-1].start()
         term = jnp.dot(dt_ref[...], c_ref[slot], preferred_element_type=F32)
         gq_ref[:, cols] = term if first else gq_in[:, cols] + term
+        if closing and last:
+            out = gd_refs[-1].at[pl.ds(split, found_ref.shape[0])]
+            leave.append(pltpu.make_async_copy(found_ref, out, sems.at[nd // SUB]))
+            leave[-1].start()
         for copy in leave:
             copy.wait()
 
@@ -165,7 +169,7 @@
     hbm = pl.BlockSpec(memory_space=pltpu.HBM)
     operands = [place, docs, *asked, ends, *sums]
     outs = nd // split
-    out_shape = [pltpu.HBM((split, width), F32)] * outs
+    out_shape = [pltpu.HBM((split + 8 if last else split, width), F32)] * outs
     out_shape += [jax.ShapeDtypeStruct((width, nq), F32), jax.ShapeDtypeStruct((8, width if last else nq), F32)]
     if first:
         line = jax.ShapeDtypeStruct((1, nq), F32)
@@ -191,7 +195,10 @@
 
 
 def all_sides(array, along):
-    return {side: moved(array, along, side) for side in (0, 2, 1, -1)}
+    sides = {}
+    for side in (0, 2, 1, -1):
+        sides[side] = moved(array, along, side)
+    return sides
 
 
 def on_device(queries, documents, log_norms, weights, positives):
@@ -230,13 +237,14 @@
     far_b = moved(terms[2][1], True, 1)
     behind = moved(jnp.concatenate([terms[-1][0][:n], terms[-1][0][n:] + far_b]), True, 1)
     ahead_a = moved(terms[1][0] + far_a, True, -1)
-    ahead_b = moved(jnp.concatenate([terms[1][1], lost]), True, -1)
+    ahead_b = moved(terms[1][1], True, -1)
     lost = lost + moved(lost, True, 1) + moved(lost, True, 2) + ahead_b[n:]
     total = terms[0][0] + jnp.concatenate([ahead_a, ahead_b[:n]]) + behind
     n = nd // 4
-    part = sum(
-        moved(jnp.concatenate([total[i * n : (i + 1) * n], lost]), False, -s) for i, s in enumerate(SIDES)
-    )
+    part = jnp.concatenate([total[:n], lost])
+    for i, side in enumerate(SIDES):
+        if side:
+            part = part + moved(jnp.concatenate([total[i * n : (i + 1) * n], lost]), False, -side)
     mine, given = part[: n // 2], part[n // 2 :]
     got = other_core(given)
     lost = given[n // 2 :] + got[n // 2 :]

time: 126 us -> 125 us (level)
  no operation moved by 1% of the time
where the time goes in v2:
time: 125 us; the launch traced here: 124 us
  waiting for transfers between devices  48.1 us (38%)
  starting transfers between devices  37.7 us (30%)
  Pallas kernels  24.5 us (20%)
  other arithmetic  7.51 us (6%)
  local copies, waits for them, and re-layouts  3.65 us (3%)
  between operations  2.7 us (2%)
    ppermute x16, waiting for transfers between devices, moved(): return lax.ppermute(array, CHIPS, route)  29 us
    pallas_call x5, Pallas kernels, fused(): pl.pallas_call(functools.partial(kernel, sizes, turn, split), in_specs=[p...  24.5 us
    ppermute x16, starting transfers between devices, moved(): return lax.ppermute(array, CHIPS, route)  17 us
    all_to_all x1, waiting for transfers between devices, on_device(): part = lax.all_to_all(part, 'z', 0, 0, tiled=True)  11.2 us
    all_to_all x1, starting transfers between devices, on_device(): lax.all_to_all(jnp.broadcast_to(documents[None], (n_z, piece, width)), 'z...  9 us
    ppermute x5, starting transfers between devices, other_core(): return lax.ppermute(array, 'core', [(0, 1), (1, 0)])  8.29 us
    all_to_all x1, waiting for transfers between devices, on_device(): lax.all_to_all(jnp.broadcast_to(documents[None], (n_z, piece, width)), 'z...  7.75 us
    all_to_all x1, starting transfers between devices, on_device(): part = lax.all_to_all(part, 'z', 0, 0, tiled=True)  3.43 us
  transfers between devices with their start and end apart: 23, of which 11 were waited for; matrix products, arithmetic and copies ran while one was open for 7% of the time, Pallas kernels for 20%

profile of v2, /device:TPU:1, one launch (start us, length us, event | category | flops | bytes accessed | tf_op | source)
XLA Modules:
  0.0 124.2 jit_solution(15497015021234518053)
XLA Ops:
  0.6 1.4 %broadcast_in_dim.6 = bf16[8,32,256]{2,1,0:T(8,128)(2,1)} broadcast(bf16[32,256]{1,0:T(8,128)(2,1)} %param.6), dimensions={1,2} | broadcast | bytes 147456 | tf_op jit(solution)/shard_map/broadcast_in_dim | solution.py:216
  2.0 9.0 %all-to-all-start = ((bf16[8,32,256]{2,1,0:T(8,128)(2,1)}), bf16[8,32,256]{2,1,0:T(8,128)(2,1)S(1)}, u32[]{:S(2)}, u32[]{:S(2)}) async-start(bf16[8,32,256]{2,1,0:T(8,128)(2,1)} %broadcast_in_dim.6), calls=%async_computation | async-start | bytes 262144 | tf_op jit(solution)/shard_map/all_to_all | solution.py:216
  11.0 7.8 %all-to-all-done = bf16[8,32,256]{2,1,0:T(8,128)(2,1)S(1)} async-done(((bf16[8,32,256]{2,1,0:T(8,128)(2,1)}), bf16[8,32,256]{2,1,0:T(8,128)(2,1)S(1)}, u32[]{:S(2)}, u32[]{:S(2)}) %all-to-all-start) | async-done | bytes 131104 | tf_op jit(solution)/shard_map/all_to_all | solution.py:216
  18.8 2.4 %collective-permute-start = (bf16[128,256]{1,0:T(8,128)(2,1)S(1)}, bf16[128,256]{1,0:T(8,128)(2,1)S(1)}, u32[]{:S(2)}, u32[]{:S(2)}) collective-permute-start(bf16[128,256]{1,0:T(8,128)(2,1)S(1)} %bitcast.20), channel_id=1, source_target_pairs={{0,8},{8,0},{1,9},{9,1},{2,10},{10,2},{3,11},{11,3},{4,12},{12,4},... | collective-permute-start | bytes 196616 | tf_op jit(solution)/shard_map/ppermute | solution.py:29
  21.2 0.1 collective-permute-start.5
  21.3 0.7 convert_element_type.12
  22.0 0.1 collective-permute-done
  22.1 1.3 %collective-permute-start.1 = (bf16[256,256]{1,0:T(8,128)(2,1)S(1)}, bf16[256,256]{1,0:T(8,128)(2,1)S(1)}, u32[]{:S(2)}, u32[]{:S(2)}) collective-permute-start(bf16[256,256]{1,0:T(8,128)(2,1)S(1)} %pad_maximum_fusion.7), channel_id=1, source_target_pairs={{0,2},{2,4},{4,6},{6,0},{8,9},{10,11},{12,13},{14,15},{1,3},{3,5},... | collective-permute-start | bytes 393224 | tf_op jit(solution)/shard_map/ppermute | solution.py:46
  23.4 1.5 %collective-permute-start.2 = (bf16[256,256]{1,0:T(8,128)(2,1)S(1)}, bf16[256,256]{1,0:T(8,128)(2,1)S(1)}, u32[]{:S(2)}, u32[]{:S(2)}) collective-permute-start(bf16[256,256]{1,0:T(8,128)(2,1)S(1)} %pad_maximum_fusion.7), channel_id=1, source_target_pairs={{0,6},{2,0},{4,2},{6,4},{8,25},{10,27},{12,29},{14,31},{1,7},{3,1}... | collective-permute-start | bytes 393224 | tf_op jit(solution)/shard_map/ppermute | solution.py:46
  24.8 1.5 %collective-permute-start.3 = (bf16[256,256]{1,0:T(8,128)(2,1)S(1)}, bf16[256,256]{1,0:T(8,128)(2,1)S(1)}, u32[]{:S(2)}, u32[]{:S(2)}) collective-permute-start(bf16[256,256]{1,0:T(8,128)(2,1)S(1)} %pad_maximum_fusion.7), channel_id=1, source_target_pairs={{0,4},{2,6},{4,0},{6,2},{8,24},{10,26},{12,28},{14,30},{1,5},{3,7}... | collective-permute-start | bytes 393224 | tf_op jit(solution)/shard_map/ppermute | solution.py:46
  26.4 1.1 collective-permute-done.1
  27.5 2.9 %collective-permute-done.3 = bf16[256,256]{1,0:T(8,128)(2,1)S(1)} collective-permute-done((bf16[256,256]{1,0:T(8,128)(2,1)S(1)}, bf16[256,256]{1,0:T(8,128)(2,1)S(1)}, u32[]{:S(2)}, u32[]{:S(2)}) %collective-permute-start.3) | collective-permute-done | bytes 131104 | tf_op jit(solution)/shard_map/ppermute | solution.py:46
  30.5 2.7 %collective-permute-start.8 = (bf16[1024,256]{1,0:T(8,128)(2,1)S(1)}, bf16[1024,256]{1,0:T(8,128)(2,1)}, u32[]{:S(2)}, u32[]{:S(2)}) collective-permute-start(bf16[1024,256]{1,0:T(8,128)(2,1)S(1)} %constant_dynamic-update-slice_fusion.refs_1_), channel_id=1, source_target_pairs={{0,16},{2,18},{4,20},{6,22},{8,12},{10,14},{12,8},{14,10},{1,17},{... | collective-permute-start | bytes 1572872 | tf_op jit(solution)/shard_map/ppermute | solution.py:46
  33.2 0.7 pad_maximum_fusion.8.refs_4_
  33.9 2.3 %collective-permute-start.6 = (f32[3,1024]{1,0:T(4,128)S(1)}, f32[3,1024]{1,0:T(4,128)S(1)}, u32[]{:S(2)}, u32[]{:S(2)}) collective-permute-start(f32[3,1024]{1,0:T(4,128)S(1)} %pad_maximum_fusion.8.refs_4_), channel_id=1, source_target_pairs={{0,8},{8,0},{1,9},{9,1},{2,10},{10,2},{3,11},{11,3},{4,12},{12,4},... | collective-permute-start | bytes 36872 | tf_op jit(solution)/shard_map/ppermute | solution.py:29
  36.2 0.7 mul.20
  37.0 1.8 %collective-permute-start.7 = (bf16[1024,256]{1,0:T(8,128)(2,1)S(1)}, bf16[1024,256]{1,0:T(8,128)(2,1)S(1)}, u32[]{:S(2)}, u32[]{:S(2)}) collective-permute-start(bf16[1024,256]{1,0:T(8,128)(2,1)S(1)} %constant_dynamic-update-slice_fusion.refs_1_), channel_id=1, source_target_pairs={{0,17},{2,19},{4,21},{6,23},{8,14},{10,8},{12,10},{14,12},{1,0},{3... | collective-permute-start | bytes 1572872 | tf_op jit(solution)/shard_map/ppermute | solution.py:46
  38.8 6.3 %fused.5 = (f32[1024,256]{1,0:T(8,128)}, f32[256,2048]{1,0:T(8,128)S(1)}, f32[8,2048]{1,0:T(8,128)S(1)}, bf16[2048,256]{1,0:T(8,128)(2,1)S(1)}, bf16[256,2048]{1...) custom-call(s32[3]{0:T(128)S(1)} %pad_add_fusion.refs_0_, ...), custom_call_target="tpu_custom_call" | custom-call | flops 3221225472 | bytes 8388608 | tf_op jit(solution)/shard_map/fused/pallas_call | solution.py:178
  45.0 5.8 %fused.6 = (f32[512,256]{1,0:T(8,128)}, f32[512,256]{1,0:T(8,128)}, f32[256,2048]{1,0:T(8,128)S(1)}, f32[8,2048]{1,0:T(8,128)S(1)}) custom-call(s32[3]{0:T(128)S(1)} %pad_add_fusion.refs_0_, bf16[1024,256]{1,0:T(8,128)(2,1)} %collective-permute-done.8.refs_1_, bf16[2048,256]{1,0:T(8,128)(2,1)S(1)} %get-tuple-element.24.refs_2_, ...), custom_call_target="tpu_custom_call", output_to_operand_aliasing={{2}: (8, {})} | custom-call | flops 3221225472 | bytes 8388608 | tf_op jit(solution)/shard_map/fused/pallas_call | solution.py:178
  51.0 0.2 collective-permute-start.4
  51.1 2.6 %collective-permute-start.10 = (f32[512,256]{1,0:T(8,128)}, f32[512,256]{1,0:T(8,128)S(1)}, u32[]{:S(2)}, u32[]{:S(2)}) collective-permute-start(f32[512,256]{1,0:T(8,128)} %get-tuple-element.40), channel_id=1, source_target_pairs={{0,17},{2,19},{4,21},{6,23},{8,14},{10,8},{12,10},{14,12},{1,0},{3... | collective-permute-start | bytes 1572872 | tf_op jit(solution)/shard_map/ppermute | solution.py:46
  53.7 5.3 %fused.7 = (f32[1024,256]{1,0:T(8,128)}, f32[256,2048]{1,0:T(8,128)S(1)}, f32[8,2048]{1,0:T(8,128)S(1)}) custom-call(s32[3]{0:T(128)S(1)} %pad_add_fusion.refs_0_, bf16[1024,256]{1,0:T(8,128)(2,1)S(1)} %collective-permute-done.7.refs_1_, bf16[2048,256]{1,0:T(8,128)(2,1)S(1)} %get-tuple-element.24.refs_2_, ...), custom_call_target="tpu_custom_call", output_to_operand_aliasing={{1}: (8, {})} | custom-call | flops 3221225472 | bytes 8388608 | tf_op jit(solution)/shard_map/fused/pallas_call | solution.py:178
  59.1 1.6 %collective-permute-done.13 = f32[512,256]{1,0:T(8,128)S(1)} collective-permute-done((f32[512,256]{1,0:T(8,128)}, f32[512,256]{1,0:T(8,128)S(1)}, u32[]{:S(2)}, u32[]{:S(2)}) %collective-permute-start.13) | collective-permute-done | bytes 524320 | tf_op jit(solution)/shard_map/ppermute | solution.py:46
  60.7 1.3 %fusion.7 = (f32[512,256]{1,0:T(8,128)S(1)}, f32[512,256]{1,0:T(8,128)S(1)}) fusion(f32[1024,256]{1,0:T(8,128)} %get-tuple-element.42, f32[512,256]{1,0:T(8,128)S(1)} %collective-permute-done.13), kind=kLoop, calls=%fused_computation.33 | loop fusion | flops 131072 | bytes 2621440 | tf_op jit(solution)/shard_map/slice | solution.py:238
  62.1 0.1 collective-permute-start.14
  62.2 4.1 %collective-permute-done.4.refs_1_ = bf16[1024,256]{1,0:T(8,128)(2,1)S(1)} collective-permute-done((bf16[1024,256]{1,0:T(8,128)(2,1)S(1)}, bf16[1024,256]{1,0:T(8,128)(2,1)S(1)}, u32[]{:S(2)}, u32[]{:S(2)}) %collective-permute-start.4) | collective-permute-done | bytes 524320 | tf_op jit(solution)/shard_map/ppermute | solution.py:46
  66.3 3.6 %fused.8 = (f32[512,256]{1,0:T(8,128)}, f32[256,2048]{1,0:T(8,128)S(1)}, f32[8,2048]{1,0:T(8,128)S(1)}) custom-call(s32[3]{0:T(128)S(1)} %pad_add_fusion.refs_0_, bf16[1024,256]{1,0:T(8,128)(2,1)S(1)} %collective-permute-done.4.refs_1_, bf16[2048,256]{1,0:T(8,128)(2,1)S(1)} %get-tuple-element.24.refs_2_, ...), custom_call_target="tpu_custom_call", output_to_operand_aliasing={{1}: (8, {})} | custom-call | flops 1610612736 | bytes 8388608 | tf_op jit(solution)/shard_map/fused/pallas_call | solution.py:178
  69.9 3.6 %fused.9 = (f32[520,256]{1,0:T(8,128)}, f32[256,2048]{1,0:T(8,128)S(1)}, f32[8,256]{1,0:T(8,128)S(1)}) custom-call(s32[3]{0:T(128)S(1)} %pad_add_fusion.refs_0_, bf16[1024,256]{1,0:T(8,128)(2,1)S(1)} %collective-permute-done.4.refs_1_, bf16[2048,256]{1,0:T(8,128)(2,1)S(1)} %get-tuple-element.24.refs_2_, ...), custom_call_target="tpu_custom_call", output_to_operand_aliasing={{1}: (8, {})} | custom-call | flops 1610612736 | bytes 8388608 | tf_op jit(solution)/shard_map/fused/pallas_call | solution.py:178
  73.8 1.5 %collective-permute-start.15 = (f32[8,256]{1,0:T(8,128)S(1)}, f32[8,256]{1,0:T(8,128)S(1)}, u32[]{:S(2)}, u32[]{:S(2)}) collective-permute-start(f32[8,256]{1,0:T(8,128)S(1)} %get-tuple-element.44), channel_id=1, source_target_pairs={{0,1},{2,3},{4,5},{6,7},{8,10},{10,12},{12,14},{14,8},{1,16},{3,18... | collective-permute-start | bytes 24584 | tf_op jit(solution)/shard_map/ppermute | solution.py:46
  75.3 1.7 %collective-permute-start.16 = (f32[8,256]{1,0:T(8,128)S(1)}, f32[8,256]{1,0:T(8,128)S(1)}, u32[]{:S(2)}, u32[]{:S(2)}) collective-permute-start(f32[8,256]{1,0:T(8,128)S(1)} %get-tuple-element.44), channel_id=1, source_target_pairs={{0,16},{2,18},{4,20},{6,22},{8,12},{10,14},{12,8},{14,10},{1,17},{... | collective-permute-start | bytes 24584 | tf_op jit(solution)/shard_map/ppermute | solution.py:46
  77.0 5.2 %collective-permute-done.12 = f32[520,256]{1,0:T(8,128)S(1)} collective-permute-done((f32[520,256]{1,0:T(8,128)}, f32[520,256]{1,0:T(8,128)S(1)}, u32[]{:S(2)}, u32[]{:S(2)}) %collective-permute-start.12) | collective-permute-done | bytes 532512 | tf_op jit(solution)/shard_map/ppermute | solution.py:46
  82.3 5.5 %collective-permute-done.11 = f32[512,256]{1,0:T(8,128)S(1)} collective-permute-done((f32[512,256]{1,0:T(8,128)S(1)}, f32[512,256]{1,0:T(8,128)S(1)}, u32[]{:S(2)}, u32[]{:S(2)}) %collective-permute-start.11) | collective-permute-done | bytes 524320 | tf_op jit(solution)/shard_map/ppermute | solution.py:46
  87.8 0.2 fusion
  88.2 0.6 collective-permute-start.17
  88.8 0.9 collective-permute-start.18
  89.7 0.4 collective-permute-start.19
  90.1 3.8 %collective-permute-done.17 = f32[264,256]{1,0:T(8,128)S(1)} collective-permute-done((f32[264,256]{1,0:T(8,128)S(1)}, f32[264,256]{1,0:T(8,128)S(1)}, u32[]{:S(2)}, u32[]{:S(2)}) %collective-permute-start.17) | collective-permute-done | bytes 270368 | tf_op jit(solution)/shard_map/ppermute | solution.py:46
  93.9 4.7 %collective-permute-done.18 = f32[264,256]{1,0:T(8,128)S(1)} collective-permute-done((f32[264,256]{1,0:T(8,128)S(1)}, f32[264,256]{1,0:T(8,128)S(1)}, u32[]{:S(2)}, u32[]{:S(2)}) %collective-permute-start.18) | collective-permute-done | bytes 270368 | tf_op jit(solution)/shard_map/ppermute | solution.py:46
  98.5 0.1 fusion.4
  98.6 3.5 %collective-permute-start.20 = (f32[136,256]{1,0:T(8,128)S(1)}, f32[136,256]{1,0:T(8,128)S(1)}, u32[]{:S(2)}, u32[]{:S(2)}) collective-permute-start(f32[136,256]{1,0:T(8,128)S(1)} %slice.78), channel_id=1, source_target_pairs={{0,8},{8,0},{1,9},{9,1},{2,10},{10,2},{3,11},{11,3},{4,12},{12,4},... | collective-permute-start | bytes 417800 | tf_op jit(solution)/shard_map/ppermute | solution.py:29
  102.2 1.1 slice.55
  103.4 0.8 pad_maximum_fusion.5
  104.1 3.4 %all-to-all-start.1 = ((f32[8,40,256]{2,1,0:T(8,128)}), f32[8,40,256]{2,1,0:T(8,128)S(1)}, u32[]{:S(2)}, u32[]{:S(2)}) async-start(f32[8,40,256]{2,1,0:T(8,128)} %pad_maximum_fusion.5), calls=%async_computation.1 | async-start | bytes 655360 | tf_op jit(solution)/shard_map/all_to_all | solution.py:255
  107.6 1.4 %fusion.1 = bf16[1024,256]{0,1:T(8,128)(2,1)S(1)} fusion(f32[256,1024]{1,0:T(8,128)} %collective-permute-done.9, f32[256,2048]{1,0:T(8,128)S(1)} %get-tuple-element.37), kind=kLoop, calls=%fused_computation.8 | loop fusion | flops 786432 | bytes 2621440 | tf_op jit(solution)/shard_map/convert_element_type | solution.py:262
  109.0 1.0 copy.13
  110.0 11.2 %all-to-all-done.1 = f32[8,40,256]{2,1,0:T(8,128)S(1)} async-done(((f32[8,40,256]{2,1,0:T(8,128)}), f32[8,40,256]{2,1,0:T(8,128)S(1)}, u32[]{:S(2)}, u32[]{:S(2)}) %all-to-all-start.1) | async-done | bytes 327712 | tf_op jit(solution)/shard_map/all_to_all | solution.py:255
  121.2 0.6 fusion.5
  121.8 0.6 slice_reduce_fusion
  (42 shorter events, 0.9 us)
Async XLA Ops:
  2.0 16.8 %all-to-all-start = ((bf16[8,32,256]{2,1,0:T(8,128)(2,1)}), bf16[8,32,256]{2,1,0:T(8,128)(2,1)S(1)}, u32[]{:S(2)}, u32[]{:S(2)}) async-start(bf16[8,32,256]{2,1,0:T(8,128)(2,1)} %broadcast_in_dim.6), calls=%async_computation | async-start | bytes 262144 | tf_op jit(solution)/shard_map/all_to_all | solution.py:216
  18.8 3.3 %collective-permute-start = (bf16[128,256]{1,0:T(8,128)(2,1)S(1)}, bf16[128,256]{1,0:T(8,128)(2,1)S(1)}, u32[]{:S(2)}, u32[]{:S(2)}) collective-permute-start(bf16[128,256]{1,0:T(8,128)(2,1)S(1)} %bitcast.20), channel_id=1, source_target_pairs={{0,8},{8,0},{1,9},{9,1},{2,10},{10,2},{3,11},{11,3},{4,12},{12,4},... | collective-permute-start | bytes 196616 | tf_op jit(solution)/shard_map/ppermute | solution.py:29
  21.2 17.6 %collective-permute-start.5 = (bf16[1024,256]{1,0:T(8,128)(2,1)}, bf16[1024,256]{1,0:T(8,128)(2,1)S(1)}, u32[]{:S(2)}, u32[]{:S(2)}) collective-permute-start(bf16[1024,256]{1,0:T(8,128)(2,1)} %refs_2_.1), channel_id=1, source_target_pairs={{0,8},{8,0},{1,9},{9,1},{2,10},{10,2},{3,11},{11,3},{4,12},{12,4},... | collective-permute-start | bytes 1572872 | tf_op jit(solution)/shard_map/ppermute | solution.py:29
  22.1 5.4 %collective-permute-start.1 = (bf16[256,256]{1,0:T(8,128)(2,1)S(1)}, bf16[256,256]{1,0:T(8,128)(2,1)S(1)}, u32[]{:S(2)}, u32[]{:S(2)}) collective-permute-start(bf16[256,256]{1,0:T(8,128)(2,1)S(1)} %pad_maximum_fusion.7), channel_id=1, source_target_pairs={{0,2},{2,4},{4,6},{6,0},{8,9},{10,11},{12,13},{14,15},{1,3},{3,5},... | collective-permute-start | bytes 393224 | tf_op jit(solution)/shard_map/ppermute | solution.py:46
  23.4 4.1 %collective-permute-start.2 = (bf16[256,256]{1,0:T(8,128)(2,1)S(1)}, bf16[256,256]{1,0:T(8,128)(2,1)S(1)}, u32[]{:S(2)}, u32[]{:S(2)}) collective-permute-start(bf16[256,256]{1,0:T(8,128)(2,1)S(1)} %pad_maximum_fusion.7), channel_id=1, source_target_pairs={{0,6},{2,0},{4,2},{6,4},{8,25},{10,27},{12,29},{14,31},{1,7},{3,1}... | collective-permute-start | bytes 393224 | tf_op jit(solution)/shard_map/ppermute | solution.py:46
  24.8 5.6 %collective-permute-start.3 = (bf16[256,256]{1,0:T(8,128)(2,1)S(1)}, bf16[256,256]{1,0:T(8,128)(2,1)S(1)}, u32[]{:S(2)}, u32[]{:S(2)}) collective-permute-start(bf16[256,256]{1,0:T(8,128)(2,1)S(1)} %pad_maximum_fusion.7), channel_id=1, source_target_pairs={{0,4},{2,6},{4,0},{6,2},{8,24},{10,26},{12,28},{14,30},{1,5},{3,7}... | collective-permute-start | bytes 393224 | tf_op jit(solution)/shard_map/ppermute | solution.py:46
  30.5 14.6 %collective-permute-start.8 = (bf16[1024,256]{1,0:T(8,128)(2,1)S(1)}, bf16[1024,256]{1,0:T(8,128)(2,1)}, u32[]{:S(2)}, u32[]{:S(2)}) collective-permute-start(bf16[1024,256]{1,0:T(8,128)(2,1)S(1)} %constant_dynamic-update-slice_fusion.refs_1_), channel_id=1, source_target_pairs={{0,16},{2,18},{4,20},{6,22},{8,12},{10,14},{12,8},{14,10},{1,17},{... | collective-permute-start | bytes 1572872 | tf_op jit(solution)/shard_map/ppermute | solution.py:46
  33.9 4.8 %collective-permute-start.6 = (f32[3,1024]{1,0:T(4,128)S(1)}, f32[3,1024]{1,0:T(4,128)S(1)}, u32[]{:S(2)}, u32[]{:S(2)}) collective-permute-start(f32[3,1024]{1,0:T(4,128)S(1)} %pad_maximum_fusion.8.refs_4_), channel_id=1, source_target_pairs={{0,8},{8,0},{1,9},{9,1},{2,10},{10,2},{3,11},{11,3},{4,12},{12,4},... | collective-permute-start | bytes 36872 | tf_op jit(solution)/shard_map/ppermute | solution.py:29
  37.0 16.7 %collective-permute-start.7 = (bf16[1024,256]{1,0:T(8,128)(2,1)S(1)}, bf16[1024,256]{1,0:T(8,128)(2,1)S(1)}, u32[]{:S(2)}, u32[]{:S(2)}) collective-permute-start(bf16[1024,256]{1,0:T(8,128)(2,1)S(1)} %constant_dynamic-update-slice_fusion.refs_1_), channel_id=1, source_target_pairs={{0,17},{2,19},{4,21},{6,23},{8,14},{10,8},{12,10},{14,12},{1,0},{3... | collective-permute-start | bytes 1572872 | tf_op jit(solution)/shard_map/ppermute | solution.py:46
  50.9 9.8 %collective-permute-start.13 = (f32[512,256]{1,0:T(8,128)}, f32[512,256]{1,0:T(8,128)S(1)}, u32[]{:S(2)}, u32[]{:S(2)}) collective-permute-start(f32[512,256]{1,0:T(8,128)} %get-tuple-element.43), channel_id=1, source_target_pairs={{0,1},{2,3},{4,5},{6,7},{8,10},{10,12},{12,14},{14,8},{1,16},{3,18... | collective-permute-start | bytes 1572872 | tf_op jit(solution)/shard_map/ppermute | solution.py:46
  51.0 15.4 %collective-permute-start.4 = (bf16[1024,256]{1,0:T(8,128)(2,1)S(1)}, bf16[1024,256]{1,0:T(8,128)(2,1)S(1)}, u32[]{:S(2)}, u32[]{:S(2)}) collective-permute-start(bf16[1024,256]{1,0:T(8,128)(2,1)S(1)} %constant_dynamic-update-slice_fusion.refs_1_), channel_id=1, source_target_pairs={{0,1},{2,3},{4,5},{6,7},{8,10},{10,12},{12,14},{14,8},{1,16},{3,18... | collective-permute-start | bytes 1572872 | tf_op jit(solution)/shard_map/ppermute | solution.py:46
  51.1 22.4 %collective-permute-start.10 = (f32[512,256]{1,0:T(8,128)}, f32[512,256]{1,0:T(8,128)S(1)}, u32[]{:S(2)}, u32[]{:S(2)}) collective-permute-start(f32[512,256]{1,0:T(8,128)} %get-tuple-element.40), channel_id=1, source_target_pairs={{0,17},{2,19},{4,21},{6,23},{8,14},{10,8},{12,10},{14,12},{1,0},{3... | collective-permute-start | bytes 1572872 | tf_op jit(solution)/shard_map/ppermute | solution.py:46
  62.1 25.7 %collective-permute-start.14 = (f32[1024,256]{1,0:T(8,128)S(1)}, f32[1024,256]{1,0:T(8,128)S(1)}, u32[]{:S(2)}, u32[]{:S(2)}) collective-permute-start(f32[1024,256]{1,0:T(8,128)S(1)} %pad_maximum_fusion), channel_id=1, source_target_pairs={{0,1},{2,3},{4,5},{6,7},{8,10},{10,12},{12,14},{14,8},{1,16},{3,18... | collective-permute-start | bytes 3145736 | tf_op jit(solution)/shard_map/ppermute | solution.py:46
  69.9 3.7 %copy-start.1 = (f32[512,256]{1,0:T(8,128)S(1)}, f32[512,256]{1,0:T(8,128)}, u32[]{:S(2)}) copy-start(f32[512,256]{1,0:T(8,128)} %get-tuple-element.39) | copy-start | bytes 1572868
  73.5 14.3 %copy-start = (f32[1024,256]{1,0:T(8,128)S(1)}, f32[1024,256]{1,0:T(8,128)}, u32[]{:S(2)}) copy-start(f32[1024,256]{1,0:T(8,128)} %get-tuple-element.38) | copy-start | bytes 3145732
  73.5 8.7 %collective-permute-start.12 = (f32[520,256]{1,0:T(8,128)}, f32[520,256]{1,0:T(8,128)S(1)}, u32[]{:S(2)}, u32[]{:S(2)}) collective-permute-start(f32[520,256]{1,0:T(8,128)} %get-tuple-element.41), channel_id=1, source_target_pairs={{0,17},{2,19},{4,21},{6,23},{8,14},{10,8},{12,10},{14,12},{1,0},{3... | collective-permute-start | bytes 1597448 | tf_op jit(solution)/shard_map/ppermute | solution.py:46
  73.7 14.1 %collective-permute-start.11 = (f32[512,256]{1,0:T(8,128)S(1)}, f32[512,256]{1,0:T(8,128)S(1)}, u32[]{:S(2)}, u32[]{:S(2)}) collective-permute-start(f32[512,256]{1,0:T(8,128)S(1)} %add.41), channel_id=1, source_target_pairs={{0,17},{2,19},{4,21},{6,23},{8,14},{10,8},{12,10},{14,12},{1,0},{3... | collective-permute-start | bytes 1572872 | tf_op jit(solution)/shard_map/ppermute | solution.py:46
  73.8 8.5 %collective-permute-start.15 = (f32[8,256]{1,0:T(8,128)S(1)}, f32[8,256]{1,0:T(8,128)S(1)}, u32[]{:S(2)}, u32[]{:S(2)}) collective-permute-start(f32[8,256]{1,0:T(8,128)S(1)} %get-tuple-element.44), channel_id=1, source_target_pairs={{0,1},{2,3},{4,5},{6,7},{8,10},{10,12},{12,14},{14,8},{1,16},{3,18... | collective-permute-start | bytes 24584 | tf_op jit(solution)/shard_map/ppermute | solution.py:46
  75.3 7.0 %collective-permute-start.16 = (f32[8,256]{1,0:T(8,128)S(1)}, f32[8,256]{1,0:T(8,128)S(1)}, u32[]{:S(2)}, u32[]{:S(2)}) collective-permute-start(f32[8,256]{1,0:T(8,128)S(1)} %get-tuple-element.44), channel_id=1, source_target_pairs={{0,16},{2,18},{4,20},{6,22},{8,12},{10,14},{12,8},{14,10},{1,17},{... | collective-permute-start | bytes 24584 | tf_op jit(solution)/shard_map/ppermute | solution.py:46
  88.2 5.7 %collective-permute-start.17 = (f32[264,256]{1,0:T(8,128)S(1)}, f32[264,256]{1,0:T(8,128)S(1)}, u32[]{:S(2)}, u32[]{:S(2)}) collective-permute-start(f32[264,256]{1,0:T(8,128)S(1)} %get-tuple-element.61), channel_id=1, source_target_pairs={{0,6},{2,0},{4,2},{6,4},{8,25},{10,27},{12,29},{14,31},{1,7},{3,1}... | collective-permute-start | bytes 811016 | tf_op jit(solution)/shard_map/ppermute | solution.py:46
  88.8 9.7 %collective-permute-start.18 = (f32[264,256]{1,0:T(8,128)S(1)}, f32[264,256]{1,0:T(8,128)S(1)}, u32[]{:S(2)}, u32[]{:S(2)}) collective-permute-start(f32[264,256]{1,0:T(8,128)S(1)} %get-tuple-element.62), channel_id=1, source_target_pairs={{0,2},{2,4},{4,6},{6,0},{8,9},{10,11},{12,13},{14,15},{1,3},{3,5},... | collective-permute-start | bytes 811016 | tf_op jit(solution)/shard_map/ppermute | solution.py:46
  89.7 8.8 %collective-permute-start.19 = (f32[264,256]{1,0:T(8,128)S(1)}, f32[264,256]{1,0:T(8,128)S(1)}, u32[]{:S(2)}, u32[]{:S(2)}) collective-permute-start(f32[264,256]{1,0:T(8,128)S(1)} %get-tuple-element.63), channel_id=1, source_target_pairs={{0,4},{2,6},{4,0},{6,2},{8,24},{10,26},{12,28},{14,30},{1,5},{3,7}... | collective-permute-start | bytes 811016 | tf_op jit(solution)/shard_map/ppermute | solution.py:46
  98.6 4.6 %collective-permute-start.20 = (f32[136,256]{1,0:T(8,128)S(1)}, f32[136,256]{1,0:T(8,128)S(1)}, u32[]{:S(2)}, u32[]{:S(2)}) collective-permute-start(f32[136,256]{1,0:T(8,128)S(1)} %slice.78), channel_id=1, source_target_pairs={{0,8},{8,0},{1,9},{9,1},{2,10},{10,2},{3,11},{11,3},{4,12},{12,4},... | collective-permute-start | bytes 417800 | tf_op jit(solution)/shard_map/ppermute | solution.py:29
  103.3 4.3 %collective-permute-start.9 = (f32[256,1024]{1,0:T(8,128)}, f32[256,1024]{1,0:T(8,128)}, u32[]{:S(2)}, u32[]{:S(2)}) collective-permute-start(f32[256,1024]{1,0:T(8,128)} %slice.55), channel_id=1, source_target_pairs={{0,8},{8,0},{1,9},{9,1},{2,10},{10,2},{3,11},{11,3},{4,12},{12,4},... | collective-permute-start | bytes 3145736 | tf_op jit(solution)/shard_map/ppermute | solution.py:29
  104.1 17.1 %all-to-all-start.1 = ((f32[8,40,256]{2,1,0:T(8,128)}), f32[8,40,256]{2,1,0:T(8,128)S(1)}, u32[]{:S(2)}, u32[]{:S(2)}) async-start(f32[8,40,256]{2,1,0:T(8,128)} %pad_maximum_fusion.5), calls=%async_computation.1 | async-start | bytes 655360 | tf_op jit(solution)/shard_map/all_to_all | solution.py:255

commit v3 on v2

--- a/solution.py
+++ b/solution.py
@@ -22,6 +22,7 @@
 SUB = 256
 SIDES = (0, 1, -1, 2)
 TURNS = ((0, 0, 4), (2, 0, 4), (-1, 0, 4), (1, 0, 2), (1, 2, 4))
+KEPT = 3
 VMEM_LIMIT = 16 << 20
 
 
@@ -64,6 +65,7 @@
 def kernel(sizes, turn, split, *refs):
     n_x, n_y, n_z = sizes
     first, last = turn == 0, turn == len(TURNS) - 1
+    kept = turn >= KEPT
     side, begin, end = TURNS[turn]
     place_ref, d_ref, *refs = refs
     if first:
@@ -128,17 +130,20 @@
         for r in range(0, nd, SUB):
             rows = slice(r, r + SUB)
             term = jnp.dot(c_ref[slot, rows, :], q, preferred_element_type=F32)
-            gd_ref[rows, :] = term if opening else gd_ref[rows, :] + term
-            if closing:
+            if not opening:
+                term = gd_ref[rows, :] + term
+            if closing and kept:
+                gd_refs[r // split][r % split : r % split + SUB, :] = term
+            else:
+                gd_ref[rows, :] = term
+            if closing and not kept:
                 out = gd_refs[r // split].at[pl.ds(r % split, SUB)]
                 leave.append(pltpu.make_async_copy(gd_ref.at[rows], out, sems.at[r // SUB]))
                 leave[-1].start()
         term = jnp.dot(dt_ref[...], c_ref[slot], preferred_element_type=F32)
         gq_ref[:, cols] = term if first else gq_in[:, cols] + term
         if closing and last:
-            out = gd_refs[-1].at[pl.ds(split, found_ref.shape[0])]
-            leave.append(pltpu.make_async_copy(found_ref, out, sems.at[nd // SUB]))
-            leave[-1].start()
+            gd_refs[-1][split:, :] = found_ref[...]
         for copy in leave:
             copy.wait()
 
@@ -169,7 +174,9 @@
     hbm = pl.BlockSpec(memory_space=pltpu.HBM)
     operands = [place, docs, *asked, ends, *sums]
     outs = nd // split
-    out_shape = [pltpu.HBM((split + 8 if last else split, width), F32)] * outs
+    kept = turn >= KEPT
+    sums_shape = (split + 8 if last else split, width)
+    out_shape = [jax.ShapeDtypeStruct(sums_shape, F32) if kept else pltpu.HBM(sums_shape, F32)] * outs
     out_shape += [jax.ShapeDtypeStruct((width, nq), F32), jax.ShapeDtypeStruct((8, width if last else nq), F32)]
     if first:
         line = jax.ShapeDtypeStruct((1, nq), F32)
@@ -178,7 +185,7 @@
     return pl.pallas_call(
         functools.partial(kernel, sizes, turn, split),
         in_specs=[pl.BlockSpec(memory_space=pltpu.SMEM), vmem, hbm if first else vmem] + [vmem] * (len(operands) - 3),
-        out_specs=[hbm] * outs + [vmem] * (len(out_shape) - outs),
+        out_specs=[vmem if kept else hbm] * outs + [vmem] * (len(out_shape) - outs),
         out_shape=out_shape,
         scratch_shapes=[
             pltpu.VMEM((width, nd), BF16),

time: 125 us -> 123 us (0.984)
  transfers between devices with their start and end apart: 23 -> 23, of which waited for: 11 -> 11; matrix products, arithmetic and copies ran while one was open for 7% -> 7% of each run, Pallas kernels for 20% -> 19%
where the time goes in v3:
time: 123 us
  waiting for transfers between devices  47.9 us (39%)
  starting transfers between devices  37.7 us (31%)
  Pallas kernels  23.4 us (19%)
  other arithmetic  7.53 us (6%)
  local copies, waits for them, and re-layouts  3.65 us (3%)
  between operations  2.68 us (2%)
    ppermute x16, waiting for transfers between devices, moved(): return lax.ppermute(array, CHIPS, route)  28.8 us
    pallas_call x5, Pallas kernels, fused(): pl.pallas_call(functools.partial(kernel, sizes, turn, split), in_specs=[p...  23.4 us
    ppermute x16, starting transfers between devices, moved(): return lax.ppermute(array, CHIPS, route)  17 us
    all_to_all x1, waiting for transfers between devices, on_device(): part = lax.all_to_all(part, 'z', 0, 0, tiled=True)  11.2 us
    all_to_all x1, starting transfers between devices, on_device(): lax.all_to_all(jnp.broadcast_to(documents[None], (n_z, piece, width)), 'z...  9 us
    ppermute x5, starting transfers between devices, other_core(): return lax.ppermute(array, 'core', [(0, 1), (1, 0)])  8.29 us
    all_to_all x1, waiting for transfers between devices, on_device(): lax.all_to_all(jnp.broadcast_to(documents[None], (n_z, piece, width)), 'z...  7.75 us
    all_to_all x1, starting transfers between devices, on_device(): part = lax.all_to_all(part, 'z', 0, 0, tiled=True)  3.43 us
  transfers between devices with their start and end apart: 23, of which 11 were waited for; matrix products, arithmetic and copies ran while one was open for 7% of the time, Pallas kernels for 19%

profile of v3, /device:TPU:1, one launch (start us, length us, event | category | flops | bytes accessed | tf_op | source)
XLA Modules:
  0.0 122.9 jit_solution(16749345873897847324)
XLA Ops:
  0.6 1.4 %broadcast_in_dim.6 = bf16[8,32,256]{2,1,0:T(8,128)(2,1)} broadcast(bf16[32,256]{1,0:T(8,128)(2,1)} %param.6), dimensions={1,2} | broadcast | bytes 147456 | tf_op jit(solution)/shard_map/broadcast_in_dim | solution.py:223
  2.0 9.0 %all-to-all-start = ((bf16[8,32,256]{2,1,0:T(8,128)(2,1)}), bf16[8,32,256]{2,1,0:T(8,128)(2,1)S(1)}, u32[]{:S(2)}, u32[]{:S(2)}) async-start(bf16[8,32,256]{2,1,0:T(8,128)(2,1)} %broadcast_in_dim.6), calls=%async_computation | async-start | bytes 262144 | tf_op jit(solution)/shard_map/all_to_all | solution.py:223
  11.0 7.8 %all-to-all-done = bf16[8,32,256]{2,1,0:T(8,128)(2,1)S(1)} async-done(((bf16[8,32,256]{2,1,0:T(8,128)(2,1)}), bf16[8,32,256]{2,1,0:T(8,128)(2,1)S(1)}, u32[]{:S(2)}, u32[]{:S(2)}) %all-to-all-start) | async-done | bytes 131104 | tf_op jit(solution)/shard_map/all_to_all | solution.py:223
  18.8 2.4 %collective-permute-start = (bf16[128,256]{1,0:T(8,128)(2,1)S(1)}, bf16[128,256]{1,0:T(8,128)(2,1)S(1)}, u32[]{:S(2)}, u32[]{:S(2)}) collective-permute-start(bf16[128,256]{1,0:T(8,128)(2,1)S(1)} %bitcast.20), channel_id=1, source_target_pairs={{0,8},{8,0},{1,9},{9,1},{2,10},{10,2},{3,11},{11,3},{4,12},{12,4},... | collective-permute-start | bytes 196616 | tf_op jit(solution)/shard_map/ppermute | solution.py:30
  21.2 0.1 collective-permute-start.5
  21.3 0.7 convert_element_type.12
  22.0 0.1 collective-permute-done
  22.1 1.3 %collective-permute-start.1 = (bf16[256,256]{1,0:T(8,128)(2,1)S(1)}, bf16[256,256]{1,0:T(8,128)(2,1)S(1)}, u32[]{:S(2)}, u32[]{:S(2)}) collective-permute-start(bf16[256,256]{1,0:T(8,128)(2,1)S(1)} %pad_maximum_fusion.7), channel_id=1, source_target_pairs={{0,2},{2,4},{4,6},{6,0},{8,9},{10,11},{12,13},{14,15},{1,3},{3,5},... | collective-permute-start | bytes 393224 | tf_op jit(solution)/shard_map/ppermute | solution.py:47
  23.4 1.5 %collective-permute-start.2 = (bf16[256,256]{1,0:T(8,128)(2,1)S(1)}, bf16[256,256]{1,0:T(8,128)(2,1)S(1)}, u32[]{:S(2)}, u32[]{:S(2)}) collective-permute-start(bf16[256,256]{1,0:T(8,128)(2,1)S(1)} %pad_maximum_fusion.7), channel_id=1, source_target_pairs={{0,6},{2,0},{4,2},{6,4},{8,25},{10,27},{12,29},{14,31},{1,7},{3,1}... | collective-permute-start | bytes 393224 | tf_op jit(solution)/shard_map/ppermute | solution.py:47
  24.8 1.5 %collective-permute-start.3 = (bf16[256,256]{1,0:T(8,128)(2,1)S(1)}, bf16[256,256]{1,0:T(8,128)(2,1)S(1)}, u32[]{:S(2)}, u32[]{:S(2)}) collective-permute-start(bf16[256,256]{1,0:T(8,128)(2,1)S(1)} %pad_maximum_fusion.7), channel_id=1, source_target_pairs={{0,4},{2,6},{4,0},{6,2},{8,24},{10,26},{12,28},{14,30},{1,5},{3,7}... | collective-permute-start | bytes 393224 | tf_op jit(solution)/shard_map/ppermute | solution.py:47
  26.4 1.1 collective-permute-done.1
  27.5 2.9 %collective-permute-done.3 = bf16[256,256]{1,0:T(8,128)(2,1)S(1)} collective-permute-done((bf16[256,256]{1,0:T(8,128)(2,1)S(1)}, bf16[256,256]{1,0:T(8,128)(2,1)S(1)}, u32[]{:S(2)}, u32[]{:S(2)}) %collective-permute-start.3) | collective-permute-done | bytes 131104 | tf_op jit(solution)/shard_map/ppermute | solution.py:47
  30.5 2.7 %collective-permute-start.8 = (bf16[1024,256]{1,0:T(8,128)(2,1)S(1)}, bf16[1024,256]{1,0:T(8,128)(2,1)}, u32[]{:S(2)}, u32[]{:S(2)}) collective-permute-start(bf16[1024,256]{1,0:T(8,128)(2,1)S(1)} %constant_dynamic-update-slice_fusion.refs_1_), channel_id=1, source_target_pairs={{0,16},{2,18},{4,20},{6,22},{8,12},{10,14},{12,8},{14,10},{1,17},{... | collective-permute-start | bytes 1572872 | tf_op jit(solution)/shard_map/ppermute | solution.py:47
  33.2 0.7 pad_maximum_fusion.8.refs_4_
  33.9 2.3 %collective-permute-start.6 = (f32[3,1024]{1,0:T(4,128)S(1)}, f32[3,1024]{1,0:T(4,128)S(1)}, u32[]{:S(2)}, u32[]{:S(2)}) collective-permute-start(f32[3,1024]{1,0:T(4,128)S(1)} %pad_maximum_fusion.8.refs_4_), channel_id=1, source_target_pairs={{0,8},{8,0},{1,9},{9,1},{2,10},{10,2},{3,11},{11,3},{4,12},{12,4},... | collective-permute-start | bytes 36872 | tf_op jit(solution)/shard_map/ppermute | solution.py:30
  36.2 0.7 mul.20
  37.0 1.8 %collective-permute-start.7 = (bf16[1024,256]{1,0:T(8,128)(2,1)S(1)}, bf16[1024,256]{1,0:T(8,128)(2,1)S(1)}, u32[]{:S(2)}, u32[]{:S(2)}) collective-permute-start(bf16[1024,256]{1,0:T(8,128)(2,1)S(1)} %constant_dynamic-update-slice_fusion.refs_1_), channel_id=1, source_target_pairs={{0,17},{2,19},{4,21},{6,23},{8,14},{10,8},{12,10},{14,12},{1,0},{3... | collective-permute-start | bytes 1572872 | tf_op jit(solution)/shard_map/ppermute | solution.py:47
  38.8 6.3 %fused.5 = (f32[1024,256]{1,0:T(8,128)}, f32[256,2048]{1,0:T(8,128)S(1)}, f32[8,2048]{1,0:T(8,128)S(1)}, bf16[2048,256]{1,0:T(8,128)(2,1)S(1)}, bf16[256,2048]{1...) custom-call(s32[3]{0:T(128)S(1)} %pad_add_fusion.refs_0_, ...), custom_call_target="tpu_custom_call" | custom-call | flops 3221225472 | bytes 8388608 | tf_op jit(solution)/shard_map/fused/pallas_call | solution.py:185
  45.1 5.8 %fused.6 = (f32[512,256]{1,0:T(8,128)}, f32[512,256]{1,0:T(8,128)}, f32[256,2048]{1,0:T(8,128)S(1)}, f32[8,2048]{1,0:T(8,128)S(1)}) custom-call(s32[3]{0:T(128)S(1)} %pad_add_fusion.refs_0_, bf16[1024,256]{1,0:T(8,128)(2,1)} %collective-permute-done.8.refs_1_, bf16[2048,256]{1,0:T(8,128)(2,1)S(1)} %get-tuple-element.24.refs_2_, ...), custom_call_target="tpu_custom_call", output_to_operand_aliasing={{2}: (8, {})} | custom-call | flops 3221225472 | bytes 8388608 | tf_op jit(solution)/shard_map/fused/pallas_call | solution.py:185
  51.0 0.2 collective-permute-start.4
  51.2 2.6 %collective-permute-start.10 = (f32[512,256]{1,0:T(8,128)}, f32[512,256]{1,0:T(8,128)S(1)}, u32[]{:S(2)}, u32[]{:S(2)}) collective-permute-start(f32[512,256]{1,0:T(8,128)} %get-tuple-element.40), channel_id=1, source_target_pairs={{0,17},{2,19},{4,21},{6,23},{8,14},{10,8},{12,10},{14,12},{1,0},{3... | collective-permute-start | bytes 1572872 | tf_op jit(solution)/shard_map/ppermute | solution.py:47
  53.7 5.3 %fused.7 = (f32[1024,256]{1,0:T(8,128)}, f32[256,2048]{1,0:T(8,128)S(1)}, f32[8,2048]{1,0:T(8,128)S(1)}) custom-call(s32[3]{0:T(128)S(1)} %pad_add_fusion.refs_0_, bf16[1024,256]{1,0:T(8,128)(2,1)S(1)} %collective-permute-done.7.refs_1_, bf16[2048,256]{1,0:T(8,128)(2,1)S(1)} %get-tuple-element.24.refs_2_, ...), custom_call_target="tpu_custom_call", output_to_operand_aliasing={{1}: (8, {})} | custom-call | flops 3221225472 | bytes 8388608 | tf_op jit(solution)/shard_map/fused/pallas_call | solution.py:185
  59.0 1.7 %collective-permute-done.13 = f32[512,256]{1,0:T(8,128)S(1)} collective-permute-done((f32[512,256]{1,0:T(8,128)}, f32[512,256]{1,0:T(8,128)S(1)}, u32[]{:S(2)}, u32[]{:S(2)}) %collective-permute-start.13) | collective-permute-done | bytes 524320 | tf_op jit(solution)/shard_map/ppermute | solution.py:47
  60.7 1.3 %fusion.7 = (f32[512,256]{1,0:T(8,128)S(1)}, f32[512,256]{1,0:T(8,128)S(1)}) fusion(f32[1024,256]{1,0:T(8,128)} %get-tuple-element.42, f32[512,256]{1,0:T(8,128)S(1)} %collective-permute-done.13), kind=kLoop, calls=%fused_computation.33 | loop fusion | flops 131072 | bytes 2621440 | tf_op jit(solution)/shard_map/slice | solution.py:245
  62.1 0.1 collective-permute-start.14
  62.2 4.1 %collective-permute-done.4.refs_1_ = bf16[1024,256]{1,0:T(8,128)(2,1)S(1)} collective-permute-done((bf16[1024,256]{1,0:T(8,128)(2,1)S(1)}, bf16[1024,256]{1,0:T(8,128)(2,1)S(1)}, u32[]{:S(2)}, u32[]{:S(2)}) %collective-permute-start.4) | collective-permute-done | bytes 524320 | tf_op jit(solution)/shard_map/ppermute | solution.py:47
  66.3 3.0 %fused.8 = (f32[512,256]{1,0:T(8,128)S(1)}, f32[256,2048]{1,0:T(8,128)S(1)}, f32[8,2048]{1,0:T(8,128)S(1)}) custom-call(s32[3]{0:T(128)S(1)} %pad_add_fusion.refs_0_, bf16[1024,256]{1,0:T(8,128)(2,1)S(1)} %collective-permute-done.4.refs_1_, bf16[2048,256]{1,0:T(8,128)(2,1)S(1)} %get-tuple-element.24.refs_2_, ...), custom_call_target="tpu_custom_call", output_to_operand_aliasing={{1}: (8, {})} | custom-call | flops 1610612736 | bytes 8388608 | tf_op jit(solution)/shard_map/fused/pallas_call | solution.py:185
  69.3 3.0 %fused.9 = (f32[520,256]{1,0:T(8,128)S(1)}, f32[256,2048]{1,0:T(8,128)S(1)}, f32[8,256]{1,0:T(8,128)S(1)}) custom-call(s32[3]{0:T(128)S(1)} %pad_add_fusion.refs_0_, bf16[1024,256]{1,0:T(8,128)(2,1)S(1)} %collective-permute-done.4.refs_1_, bf16[2048,256]{1,0:T(8,128)(2,1)S(1)} %get-tuple-element.24.refs_2_, ...), custom_call_target="tpu_custom_call", output_to_operand_aliasing={{1}: (8, {})} | custom-call | flops 1610612736 | bytes 8388608 | tf_op jit(solution)/shard_map/fused/pallas_call | solution.py:185
  72.6 1.5 %collective-permute-start.15 = (f32[8,256]{1,0:T(8,128)S(1)}, f32[8,256]{1,0:T(8,128)S(1)}, u32[]{:S(2)}, u32[]{:S(2)}) collective-permute-start(f32[8,256]{1,0:T(8,128)S(1)} %get-tuple-element.44), channel_id=1, source_target_pairs={{0,1},{2,3},{4,5},{6,7},{8,10},{10,12},{12,14},{14,8},{1,16},{3,18... | collective-permute-start | bytes 24584 | tf_op jit(solution)/shard_map/ppermute | solution.py:47
  74.1 1.7 %collective-permute-start.16 = (f32[8,256]{1,0:T(8,128)S(1)}, f32[8,256]{1,0:T(8,128)S(1)}, u32[]{:S(2)}, u32[]{:S(2)}) collective-permute-start(f32[8,256]{1,0:T(8,128)S(1)} %get-tuple-element.44), channel_id=1, source_target_pairs={{0,16},{2,18},{4,20},{6,22},{8,12},{10,14},{12,8},{14,10},{1,17},{... | collective-permute-start | bytes 24584 | tf_op jit(solution)/shard_map/ppermute | solution.py:47
  75.8 5.0 %collective-permute-done.12 = f32[520,256]{1,0:T(8,128)S(1)} collective-permute-done((f32[520,256]{1,0:T(8,128)S(1)}, f32[520,256]{1,0:T(8,128)S(1)}, u32[]{:S(2)}, u32[]{:S(2)}) %collective-permute-start.12) | collective-permute-done | bytes 532512 | tf_op jit(solution)/shard_map/ppermute | solution.py:47
  80.9 5.5 %collective-permute-done.11 = f32[512,256]{1,0:T(8,128)S(1)} collective-permute-done((f32[512,256]{1,0:T(8,128)S(1)}, f32[512,256]{1,0:T(8,128)S(1)}, u32[]{:S(2)}, u32[]{:S(2)}) %collective-permute-start.11) | collective-permute-done | bytes 524320 | tf_op jit(solution)/shard_map/ppermute | solution.py:47
  86.5 0.2 fusion
  86.8 0.6 collective-permute-start.17
  87.5 0.9 collective-permute-start.18
  88.4 0.4 collective-permute-start.19
  88.7 3.8 %collective-permute-done.17 = f32[264,256]{1,0:T(8,128)S(1)} collective-permute-done((f32[264,256]{1,0:T(8,128)S(1)}, f32[264,256]{1,0:T(8,128)S(1)}, u32[]{:S(2)}, u32[]{:S(2)}) %collective-permute-start.17) | collective-permute-done | bytes 270368 | tf_op jit(solution)/shard_map/ppermute | solution.py:47
  92.5 4.7 %collective-permute-done.18 = f32[264,256]{1,0:T(8,128)S(1)} collective-permute-done((f32[264,256]{1,0:T(8,128)S(1)}, f32[264,256]{1,0:T(8,128)S(1)}, u32[]{:S(2)}, u32[]{:S(2)}) %collective-permute-start.18) | collective-permute-done | bytes 270368 | tf_op jit(solution)/shard_map/ppermute | solution.py:47
  97.2 0.1 fusion.4
  97.3 3.5 %collective-permute-start.20 = (f32[136,256]{1,0:T(8,128)S(1)}, f32[136,256]{1,0:T(8,128)S(1)}, u32[]{:S(2)}, u32[]{:S(2)}) collective-permute-start(f32[136,256]{1,0:T(8,128)S(1)} %slice.78), channel_id=1, source_target_pairs={{0,8},{8,0},{1,9},{9,1},{2,10},{10,2},{3,11},{11,3},{4,12},{12,4},... | collective-permute-start | bytes 417800 | tf_op jit(solution)/shard_map/ppermute | solution.py:30
  100.8 1.1 slice.55
  102.0 0.7 pad_maximum_fusion.5
  102.8 3.4 %all-to-all-start.1 = ((f32[8,40,256]{2,1,0:T(8,128)}), f32[8,40,256]{2,1,0:T(8,128)S(1)}, u32[]{:S(2)}, u32[]{:S(2)}) async-start(f32[8,40,256]{2,1,0:T(8,128)} %pad_maximum_fusion.5), calls=%async_computation.1 | async-start | bytes 655360 | tf_op jit(solution)/shard_map/all_to_all | solution.py:262
  106.2 1.4 %fusion.1 = bf16[1024,256]{0,1:T(8,128)(2,1)S(1)} fusion(f32[256,1024]{1,0:T(8,128)} %collective-permute-done.9, f32[256,2048]{1,0:T(8,128)S(1)} %get-tuple-element.37), kind=kLoop, calls=%fused_computation.8 | loop fusion | flops 786432 | bytes 2621440 | tf_op jit(solution)/shard_map/convert_element_type | solution.py:269
  107.7 1.0 copy.13
  108.7 11.2 %all-to-all-done.1 = f32[8,40,256]{2,1,0:T(8,128)S(1)} async-done(((f32[8,40,256]{2,1,0:T(8,128)}), f32[8,40,256]{2,1,0:T(8,128)S(1)}, u32[]{:S(2)}, u32[]{:S(2)}) %all-to-all-start.1) | async-done | bytes 327712 | tf_op jit(solution)/shard_map/all_to_all | solution.py:262
  119.9 0.6 fusion.5
  120.5 0.6 slice_reduce_fusion
  (40 shorter events, 0.9 us)
Async XLA Ops:
  2.0 16.8 %all-to-all-start = ((bf16[8,32,256]{2,1,0:T(8,128)(2,1)}), bf16[8,32,256]{2,1,0:T(8,128)(2,1)S(1)}, u32[]{:S(2)}, u32[]{:S(2)}) async-start(bf16[8,32,256]{2,1,0:T(8,128)(2,1)} %broadcast_in_dim.6), calls=%async_computation | async-start | bytes 262144 | tf_op jit(solution)/shard_map/all_to_all | solution.py:223
  18.8 3.3 %collective-permute-start = (bf16[128,256]{1,0:T(8,128)(2,1)S(1)}, bf16[128,256]{1,0:T(8,128)(2,1)S(1)}, u32[]{:S(2)}, u32[]{:S(2)}) collective-permute-start(bf16[128,256]{1,0:T(8,128)(2,1)S(1)} %bitcast.20), channel_id=1, source_target_pairs={{0,8},{8,0},{1,9},{9,1},{2,10},{10,2},{3,11},{11,3},{4,12},{12,4},... | collective-permute-start | bytes 196616 | tf_op jit(solution)/shard_map/ppermute | solution.py:30
  21.2 17.6 %collective-permute-start.5 = (bf16[1024,256]{1,0:T(8,128)(2,1)}, bf16[1024,256]{1,0:T(8,128)(2,1)S(1)}, u32[]{:S(2)}, u32[]{:S(2)}) collective-permute-start(bf16[1024,256]{1,0:T(8,128)(2,1)} %refs_2_.1), channel_id=1, source_target_pairs={{0,8},{8,0},{1,9},{9,1},{2,10},{10,2},{3,11},{11,3},{4,12},{12,4},... | collective-permute-start | bytes 1572872 | tf_op jit(solution)/shard_map/ppermute | solution.py:30
  22.1 5.4 %collective-permute-start.1 = (bf16[256,256]{1,0:T(8,128)(2,1)S(1)}, bf16[256,256]{1,0:T(8,128)(2,1)S(1)}, u32[]{:S(2)}, u32[]{:S(2)}) collective-permute-start(bf16[256,256]{1,0:T(8,128)(2,1)S(1)} %pad_maximum_fusion.7), channel_id=1, source_target_pairs={{0,2},{2,4},{4,6},{6,0},{8,9},{10,11},{12,13},{14,15},{1,3},{3,5},... | collective-permute-start | bytes 393224 | tf_op jit(solution)/shard_map/ppermute | solution.py:47
  23.4 4.1 %collective-permute-start.2 = (bf16[256,256]{1,0:T(8,128)(2,1)S(1)}, bf16[256,256]{1,0:T(8,128)(2,1)S(1)}, u32[]{:S(2)}, u32[]{:S(2)}) collective-permute-start(bf16[256,256]{1,0:T(8,128)(2,1)S(1)} %pad_maximum_fusion.7), channel_id=1, source_target_pairs={{0,6},{2,0},{4,2},{6,4},{8,25},{10,27},{12,29},{14,31},{1,7},{3,1}... | collective-permute-start | bytes 393224 | tf_op jit(solution)/shard_map/ppermute | solution.py:47
  24.8 5.6 %collective-permute-start.3 = (bf16[256,256]{1,0:T(8,128)(2,1)S(1)}, bf16[256,256]{1,0:T(8,128)(2,1)S(1)}, u32[]{:S(2)}, u32[]{:S(2)}) collective-permute-start(bf16[256,256]{1,0:T(8,128)(2,1)S(1)} %pad_maximum_fusion.7), channel_id=1, source_target_pairs={{0,4},{2,6},{4,0},{6,2},{8,24},{10,26},{12,28},{14,30},{1,5},{3,7}... | collective-permute-start | bytes 393224 | tf_op jit(solution)/shard_map/ppermute | solution.py:47
  30.5 14.6 %collective-permute-start.8 = (bf16[1024,256]{1,0:T(8,128)(2,1)S(1)}, bf16[1024,256]{1,0:T(8,128)(2,1)}, u32[]{:S(2)}, u32[]{:S(2)}) collective-permute-start(bf16[1024,256]{1,0:T(8,128)(2,1)S(1)} %constant_dynamic-update-slice_fusion.refs_1_), channel_id=1, source_target_pairs={{0,16},{2,18},{4,20},{6,22},{8,12},{10,14},{12,8},{14,10},{1,17},{... | collective-permute-start | bytes 1572872 | tf_op jit(solution)/shard_map/ppermute | solution.py:47
  33.9 4.8 %collective-permute-start.6 = (f32[3,1024]{1,0:T(4,128)S(1)}, f32[3,1024]{1,0:T(4,128)S(1)}, u32[]{:S(2)}, u32[]{:S(2)}) collective-permute-start(f32[3,1024]{1,0:T(4,128)S(1)} %pad_maximum_fusion.8.refs_4_), channel_id=1, source_target_pairs={{0,8},{8,0},{1,9},{9,1},{2,10},{10,2},{3,11},{11,3},{4,12},{12,4},... | collective-permute-start | bytes 36872 | tf_op jit(solution)/shard_map/ppermute | solution.py:30
  37.0 16.7 %collective-permute-start.7 = (bf16[1024,256]{1,0:T(8,128)(2,1)S(1)}, bf16[1024,256]{1,0:T(8,128)(2,1)S(1)}, u32[]{:S(2)}, u32[]{:S(2)}) collective-permute-start(bf16[1024,256]{1,0:T(8,128)(2,1)S(1)} %constant_dynamic-update-slice_fusion.refs_1_), channel_id=1, source_target_pairs={{0,17},{2,19},{4,21},{6,23},{8,14},{10,8},{12,10},{14,12},{1,0},{3... | collective-permute-start | bytes 1572872 | tf_op jit(solution)/shard_map/ppermute | solution.py:47
  50.9 9.8 %collective-permute-start.13 = (f32[512,256]{1,0:T(8,128)}, f32[512,256]{1,0:T(8,128)S(1)}, u32[]{:S(2)}, u32[]{:S(2)}) collective-permute-start(f32[512,256]{1,0:T(8,128)} %get-tuple-element.43), channel_id=1, source_target_pairs={{0,1},{2,3},{4,5},{6,7},{8,10},{10,12},{12,14},{14,8},{1,16},{3,18... | collective-permute-start | bytes 1572872 | tf_op jit(solution)/shard_map/ppermute | solution.py:47
  51.0 15.4 %collective-permute-start.4 = (bf16[1024,256]{1,0:T(8,128)(2,1)S(1)}, bf16[1024,256]{1,0:T(8,128)(2,1)S(1)}, u32[]{:S(2)}, u32[]{:S(2)}) collective-permute-start(bf16[1024,256]{1,0:T(8,128)(2,1)S(1)} %constant_dynamic-update-slice_fusion.refs_1_), channel_id=1, source_target_pairs={{0,1},{2,3},{4,5},{6,7},{8,10},{10,12},{12,14},{14,8},{1,16},{3,18... | collective-permute-start | bytes 1572872 | tf_op jit(solution)/shard_map/ppermute | solution.py:47
  51.2 21.3 %collective-permute-start.10 = (f32[512,256]{1,0:T(8,128)}, f32[512,256]{1,0:T(8,128)S(1)}, u32[]{:S(2)}, u32[]{:S(2)}) collective-permute-start(f32[512,256]{1,0:T(8,128)} %get-tuple-element.40), channel_id=1, source_target_pairs={{0,17},{2,19},{4,21},{6,23},{8,14},{10,8},{12,10},{14,12},{1,0},{3... | collective-permute-start | bytes 1572872 | tf_op jit(solution)/shard_map/ppermute | solution.py:47
  62.1 24.4 %collective-permute-start.14 = (f32[1024,256]{1,0:T(8,128)S(1)}, f32[1024,256]{1,0:T(8,128)S(1)}, u32[]{:S(2)}, u32[]{:S(2)}) collective-permute-start(f32[1024,256]{1,0:T(8,128)S(1)} %pad_maximum_fusion), channel_id=1, source_target_pairs={{0,1},{2,3},{4,5},{6,7},{8,10},{10,12},{12,14},{14,8},{1,16},{3,18... | collective-permute-start | bytes 3145736 | tf_op jit(solution)/shard_map/ppermute | solution.py:47
  72.3 14.1 %copy-start = (f32[1024,256]{1,0:T(8,128)S(1)}, f32[1024,256]{1,0:T(8,128)}, u32[]{:S(2)}) copy-start(f32[1024,256]{1,0:T(8,128)} %get-tuple-element.38) | copy-start | bytes 3145732
  72.4 8.5 %collective-permute-start.12 = (f32[520,256]{1,0:T(8,128)S(1)}, f32[520,256]{1,0:T(8,128)S(1)}, u32[]{:S(2)}, u32[]{:S(2)}) collective-permute-start(f32[520,256]{1,0:T(8,128)S(1)} %get-tuple-element.41), channel_id=1, source_target_pairs={{0,17},{2,19},{4,21},{6,23},{8,14},{10,8},{12,10},{14,12},{1,0},{3... | collective-permute-start | bytes 1597448 | tf_op jit(solution)/shard_map/ppermute | solution.py:47
  72.5 13.9 %collective-permute-start.11 = (f32[512,256]{1,0:T(8,128)S(1)}, f32[512,256]{1,0:T(8,128)S(1)}, u32[]{:S(2)}, u32[]{:S(2)}) collective-permute-start(f32[512,256]{1,0:T(8,128)S(1)} %add.41), channel_id=1, source_target_pairs={{0,17},{2,19},{4,21},{6,23},{8,14},{10,8},{12,10},{14,12},{1,0},{3... | collective-permute-start | bytes 1572872 | tf_op jit(solution)/shard_map/ppermute | solution.py:47
  72.6 8.3 %collective-permute-start.15 = (f32[8,256]{1,0:T(8,128)S(1)}, f32[8,256]{1,0:T(8,128)S(1)}, u32[]{:S(2)}, u32[]{:S(2)}) collective-permute-start(f32[8,256]{1,0:T(8,128)S(1)} %get-tuple-element.44), channel_id=1, source_target_pairs={{0,1},{2,3},{4,5},{6,7},{8,10},{10,12},{12,14},{14,8},{1,16},{3,18... | collective-permute-start | bytes 24584 | tf_op jit(solution)/shard_map/ppermute | solution.py:47
  74.1 6.8 %collective-permute-start.16 = (f32[8,256]{1,0:T(8,128)S(1)}, f32[8,256]{1,0:T(8,128)S(1)}, u32[]{:S(2)}, u32[]{:S(2)}) collective-permute-start(f32[8,256]{1,0:T(8,128)S(1)} %get-tuple-element.44), channel_id=1, source_target_pairs={{0,16},{2,18},{4,20},{6,22},{8,12},{10,14},{12,8},{14,10},{1,17},{... | collective-permute-start | bytes 24584 | tf_op jit(solution)/shard_map/ppermute | solution.py:47
  86.8 5.7 %collective-permute-start.17 = (f32[264,256]{1,0:T(8,128)S(1)}, f32[264,256]{1,0:T(8,128)S(1)}, u32[]{:S(2)}, u32[]{:S(2)}) collective-permute-start(f32[264,256]{1,0:T(8,128)S(1)} %get-tuple-element.61), channel_id=1, source_target_pairs={{0,6},{2,0},{4,2},{6,4},{8,25},{10,27},{12,29},{14,31},{1,7},{3,1}... | collective-permute-start | bytes 811016 | tf_op jit(solution)/shard_map/ppermute | solution.py:47
  87.5 9.7 %collective-permute-start.18 = (f32[264,256]{1,0:T(8,128)S(1)}, f32[264,256]{1,0:T(8,128)S(1)}, u32[]{:S(2)}, u32[]{:S(2)}) collective-permute-start(f32[264,256]{1,0:T(8,128)S(1)} %get-tuple-element.62), channel_id=1, source_target_pairs={{0,2},{2,4},{4,6},{6,0},{8,9},{10,11},{12,13},{14,15},{1,3},{3,5},... | collective-permute-start | bytes 811016 | tf_op jit(solution)/shard_map/ppermute | solution.py:47
  88.4 8.8 %collective-permute-start.19 = (f32[264,256]{1,0:T(8,128)S(1)}, f32[264,256]{1,0:T(8,128)S(1)}, u32[]{:S(2)}, u32[]{:S(2)}) collective-permute-start(f32[264,256]{1,0:T(8,128)S(1)} %get-tuple-element.63), channel_id=1, source_target_pairs={{0,4},{2,6},{4,0},{6,2},{8,24},{10,26},{12,28},{14,30},{1,5},{3,7}... | collective-permute-start | bytes 811016 | tf_op jit(solution)/shard_map/ppermute | solution.py:47
  97.3 4.6 %collective-permute-start.20 = (f32[136,256]{1,0:T(8,128)S(1)}, f32[136,256]{1,0:T(8,128)S(1)}, u32[]{:S(2)}, u32[]{:S(2)}) collective-permute-start(f32[136,256]{1,0:T(8,128)S(1)} %slice.78), channel_id=1, source_target_pairs={{0,8},{8,0},{1,9},{9,1},{2,10},{10,2},{3,11},{11,3},{4,12},{12,4},... | collective-permute-start | bytes 417800 | tf_op jit(solution)/shard_map/ppermute | solution.py:30
  101.9 4.3 %collective-permute-start.9 = (f32[256,1024]{1,0:T(8,128)}, f32[256,1024]{1,0:T(8,128)}, u32[]{:S(2)}, u32[]{:S(2)}) collective-permute-start(f32[256,1024]{1,0:T(8,128)} %slice.55), channel_id=1, source_target_pairs={{0,8},{8,0},{1,9},{9,1},{2,10},{10,2},{3,11},{11,3},{4,12},{12,4},... | collective-permute-start | bytes 3145736 | tf_op jit(solution)/shard_map/ppermute | solution.py:30
  102.8 17.1 %all-to-all-start.1 = ((f32[8,40,256]{2,1,0:T(8,128)}), f32[8,40,256]{2,1,0:T(8,128)S(1)}, u32[]{:S(2)}, u32[]{:S(2)}) async-start(f32[8,40,256]{2,1,0:T(8,128)} %pad_maximum_fusion.5), calls=%async_computation.1 | async-start | bytes 655360 | tf_op jit(solution)/shard_map/all_to_all | solution.py:262

commit v4 on v3

--- a/solution.py
+++ b/solution.py
@@ -257,12 +257,16 @@
     lost = given[n // 2 :] + got[n // 2 :]
     got = got[: n // 2]
     low, high = jnp.where(core == 0, mine, got), jnp.where(core == 0, got, mine)
-    part = jnp.concatenate([low, high]).reshape(n_z, piece, width)
-    part = jnp.concatenate([part, jnp.broadcast_to(lost[None], (n_z, 8, width))], 1)
+    fold = width // 2
+    part = jnp.concatenate([low, high])
+    sides = [part[:, i : i + fold].reshape(n_z, piece, fold) for i in (0, fold)]
+    lost = lost[:, :fold] + lost[:, fold:]
+    part = jnp.concatenate([*sides, jnp.broadcast_to(lost[None], (n_z, 8, fold))], 1)
     part = lax.all_to_all(part, "z", 0, 0, tiled=True)
-    part = part.sum(0)
-    grad_documents = (part[:piece] * 0.0625).astype(BF16)
-    loss = jnp.sum(part[piece:]) / total_q
+    loss = jnp.sum(part[:, 2 * piece :]) / total_q
+    part = part[:, : 2 * piece].sum(0)
+    part = jnp.concatenate([part[:piece], part[piece:]], 1)
+    grad_documents = (part * 0.0625).astype(BF16)
 
     other_grad = grad_q[:, own:]
     other_grad = other_core(other_grad)

time: 123 us -> 123 us (level)
  no operation moved by 1% of the time
where the time goes in v4:
time: 123 us; the launch traced here: 122 us
  waiting for transfers between devices  47.1 us (38%)
  starting transfers between devices  37.7 us (31%)
  Pallas kernels  23.4 us (19%)
  other arithmetic  7.53 us (6%)
  local copies, waits for them, and re-layouts  3.63 us (3%)
  between operations  2.7 us (2%)
    ppermute x16, waiting for transfers between devices, moved(): return lax.ppermute(array, CHIPS, route)  28.8 us
    pallas_call x5, Pallas kernels, fused(): pl.pallas_call(functools.partial(kernel, sizes, turn, split), in_specs=[p...  23.4 us
    ppermute x16, starting transfers between devices, moved(): return lax.ppermute(array, CHIPS, route)  17 us
    all_to_all x1, waiting for transfers between devices, on_device(): part = lax.all_to_all(part, 'z', 0, 0, tiled=True)  10.4 us
    all_to_all x1, starting transfers between devices, on_device(): lax.all_to_all(jnp.broadcast_to(documents[None], (n_z, piece, width)), 'z...  9 us
    ppermute x5, starting transfers between devices, other_core(): return lax.ppermute(array, 'core', [(0, 1), (1, 0)])  8.29 us
    all_to_all x1, waiting for transfers between devices, on_device(): lax.all_to_all(jnp.broadcast_to(documents[None], (n_z, piece, width)), 'z...  7.75 us
    all_to_all x1, starting transfers between devices, on_device(): part = lax.all_to_all(part, 'z', 0, 0, tiled=True)  3.42 us
  transfers between devices with their start and end apart: 23, of which 11 were waited for; matrix products, arithmetic and copies ran while one was open for 7% of the time, Pallas kernels for 19%

profile of v4, /device:TPU:1, one launch (start us, length us, event | category | flops | bytes accessed | tf_op | source)
XLA Modules:
  0.0 122.1 jit_solution(4137228653546825128)
XLA Ops:
  0.6 1.4 %broadcast_in_dim.6 = bf16[8,32,256]{2,1,0:T(8,128)(2,1)} broadcast(bf16[32,256]{1,0:T(8,128)(2,1)} %param.6), dimensions={1,2} | broadcast | bytes 147456 | tf_op jit(solution)/shard_map/broadcast_in_dim | solution.py:223
  2.0 9.0 %all-to-all-start = ((bf16[8,32,256]{2,1,0:T(8,128)(2,1)}), bf16[8,32,256]{2,1,0:T(8,128)(2,1)S(1)}, u32[]{:S(2)}, u32[]{:S(2)}) async-start(bf16[8,32,256]{2,1,0:T(8,128)(2,1)} %broadcast_in_dim.6), calls=%async_computation | async-start | bytes 262144 | tf_op jit(solution)/shard_map/all_to_all | solution.py:223
  11.0 7.8 %all-to-all-done = bf16[8,32,256]{2,1,0:T(8,128)(2,1)S(1)} async-done(((bf16[8,32,256]{2,1,0:T(8,128)(2,1)}), bf16[8,32,256]{2,1,0:T(8,128)(2,1)S(1)}, u32[]{:S(2)}, u32[]{:S(2)}) %all-to-all-start) | async-done | bytes 131104 | tf_op jit(solution)/shard_map/all_to_all | solution.py:223
  18.8 2.4 %collective-permute-start = (bf16[128,256]{1,0:T(8,128)(2,1)S(1)}, bf16[128,256]{1,0:T(8,128)(2,1)S(1)}, u32[]{:S(2)}, u32[]{:S(2)}) collective-permute-start(bf16[128,256]{1,0:T(8,128)(2,1)S(1)} %bitcast.22), channel_id=1, source_target_pairs={{0,8},{8,0},{1,9},{9,1},{2,10},{10,2},{3,11},{11,3},{4,12},{12,4},... | collective-permute-start | bytes 196616 | tf_op jit(solution)/shard_map/ppermute | solution.py:30
  21.2 0.1 collective-permute-start.5
  21.3 0.7 convert_element_type.12
  22.0 0.1 collective-permute-done
  22.1 1.3 %collective-permute-start.1 = (bf16[256,256]{1,0:T(8,128)(2,1)S(1)}, bf16[256,256]{1,0:T(8,128)(2,1)S(1)}, u32[]{:S(2)}, u32[]{:S(2)}) collective-permute-start(bf16[256,256]{1,0:T(8,128)(2,1)S(1)} %pad_maximum_fusion.7), channel_id=1, source_target_pairs={{0,2},{2,4},{4,6},{6,0},{8,9},{10,11},{12,13},{14,15},{1,3},{3,5},... | collective-permute-start | bytes 393224 | tf_op jit(solution)/shard_map/ppermute | solution.py:47
  23.4 1.5 %collective-permute-start.2 = (bf16[256,256]{1,0:T(8,128)(2,1)S(1)}, bf16[256,256]{1,0:T(8,128)(2,1)S(1)}, u32[]{:S(2)}, u32[]{:S(2)}) collective-permute-start(bf16[256,256]{1,0:T(8,128)(2,1)S(1)} %pad_maximum_fusion.7), channel_id=1, source_target_pairs={{0,6},{2,0},{4,2},{6,4},{8,25},{10,27},{12,29},{14,31},{1,7},{3,1}... | collective-permute-start | bytes 393224 | tf_op jit(solution)/shard_map/ppermute | solution.py:47
  24.8 1.5 %collective-permute-start.3 = (bf16[256,256]{1,0:T(8,128)(2,1)S(1)}, bf16[256,256]{1,0:T(8,128)(2,1)S(1)}, u32[]{:S(2)}, u32[]{:S(2)}) collective-permute-start(bf16[256,256]{1,0:T(8,128)(2,1)S(1)} %pad_maximum_fusion.7), channel_id=1, source_target_pairs={{0,4},{2,6},{4,0},{6,2},{8,24},{10,26},{12,28},{14,30},{1,5},{3,7}... | collective-permute-start | bytes 393224 | tf_op jit(solution)/shard_map/ppermute | solution.py:47
  26.4 1.1 collective-permute-done.1
  27.5 2.9 %collective-permute-done.3 = bf16[256,256]{1,0:T(8,128)(2,1)S(1)} collective-permute-done((bf16[256,256]{1,0:T(8,128)(2,1)S(1)}, bf16[256,256]{1,0:T(8,128)(2,1)S(1)}, u32[]{:S(2)}, u32[]{:S(2)}) %collective-permute-start.3) | collective-permute-done | bytes 131104 | tf_op jit(solution)/shard_map/ppermute | solution.py:47
  30.5 2.7 %collective-permute-start.8 = (bf16[1024,256]{1,0:T(8,128)(2,1)S(1)}, bf16[1024,256]{1,0:T(8,128)(2,1)}, u32[]{:S(2)}, u32[]{:S(2)}) collective-permute-start(bf16[1024,256]{1,0:T(8,128)(2,1)S(1)} %constant_dynamic-update-slice_fusion.refs_1_), channel_id=1, source_target_pairs={{0,16},{2,18},{4,20},{6,22},{8,12},{10,14},{12,8},{14,10},{1,17},{... | collective-permute-start | bytes 1572872 | tf_op jit(solution)/shard_map/ppermute | solution.py:47
  33.2 0.7 pad_maximum_fusion.8.refs_4_
  33.9 2.3 %collective-permute-start.6 = (f32[3,1024]{1,0:T(4,128)S(1)}, f32[3,1024]{1,0:T(4,128)S(1)}, u32[]{:S(2)}, u32[]{:S(2)}) collective-permute-start(f32[3,1024]{1,0:T(4,128)S(1)} %pad_maximum_fusion.8.refs_4_), channel_id=1, source_target_pairs={{0,8},{8,0},{1,9},{9,1},{2,10},{10,2},{3,11},{11,3},{4,12},{12,4},... | collective-permute-start | bytes 36872 | tf_op jit(solution)/shard_map/ppermute | solution.py:30
  36.2 0.7 mul.20
  37.0 1.8 %collective-permute-start.7 = (bf16[1024,256]{1,0:T(8,128)(2,1)S(1)}, bf16[1024,256]{1,0:T(8,128)(2,1)S(1)}, u32[]{:S(2)}, u32[]{:S(2)}) collective-permute-start(bf16[1024,256]{1,0:T(8,128)(2,1)S(1)} %constant_dynamic-update-slice_fusion.refs_1_), channel_id=1, source_target_pairs={{0,17},{2,19},{4,21},{6,23},{8,14},{10,8},{12,10},{14,12},{1,0},{3... | collective-permute-start | bytes 1572872 | tf_op jit(solution)/shard_map/ppermute | solution.py:47
  38.8 6.3 %fused.5 = (f32[1024,256]{1,0:T(8,128)}, f32[256,2048]{1,0:T(8,128)S(1)}, f32[8,2048]{1,0:T(8,128)S(1)}, bf16[2048,256]{1,0:T(8,128)(2,1)S(1)}, bf16[256,2048]{1...) custom-call(s32[3]{0:T(128)S(1)} %pad_add_fusion.refs_0_, ...), custom_call_target="tpu_custom_call" | custom-call | flops 3221225472 | bytes 8388608 | tf_op jit(solution)/shard_map/fused/pallas_call | solution.py:185
  45.0 5.8 %fused.6 = (f32[512,256]{1,0:T(8,128)}, f32[512,256]{1,0:T(8,128)}, f32[256,2048]{1,0:T(8,128)S(1)}, f32[8,2048]{1,0:T(8,128)S(1)}) custom-call(s32[3]{0:T(128)S(1)} %pad_add_fusion.refs_0_, bf16[1024,256]{1,0:T(8,128)(2,1)} %collective-permute-done.8.refs_1_, bf16[2048,256]{1,0:T(8,128)(2,1)S(1)} %get-tuple-element.24.refs_2_, ...), custom_call_target="tpu_custom_call", output_to_operand_aliasing={{2}: (8, {})} | custom-call | flops 3221225472 | bytes 8388608 | tf_op jit(solution)/shard_map/fused/pallas_call | solution.py:185
  51.0 0.2 collective-permute-start.4
  51.1 2.6 %collective-permute-start.10 = (f32[512,256]{1,0:T(8,128)}, f32[512,256]{1,0:T(8,128)S(1)}, u32[]{:S(2)}, u32[]{:S(2)}) collective-permute-start(f32[512,256]{1,0:T(8,128)} %get-tuple-element.40), channel_id=1, source_target_pairs={{0,17},{2,19},{4,21},{6,23},{8,14},{10,8},{12,10},{14,12},{1,0},{3... | collective-permute-start | bytes 1572872 | tf_op jit(solution)/shard_map/ppermute | solution.py:47
  53.7 5.3 %fused.7 = (f32[1024,256]{1,0:T(8,128)}, f32[256,2048]{1,0:T(8,128)S(1)}, f32[8,2048]{1,0:T(8,128)S(1)}) custom-call(s32[3]{0:T(128)S(1)} %pad_add_fusion.refs_0_, bf16[1024,256]{1,0:T(8,128)(2,1)S(1)} %collective-permute-done.7.refs_1_, bf16[2048,256]{1,0:T(8,128)(2,1)S(1)} %get-tuple-element.24.refs_2_, ...), custom_call_target="tpu_custom_call", output_to_operand_aliasing={{1}: (8, {})} | custom-call | flops 3221225472 | bytes 8388608 | tf_op jit(solution)/shard_map/fused/pallas_call | solution.py:185
  59.0 1.6 %collective-permute-done.13 = f32[512,256]{1,0:T(8,128)S(1)} collective-permute-done((f32[512,256]{1,0:T(8,128)}, f32[512,256]{1,0:T(8,128)S(1)}, u32[]{:S(2)}, u32[]{:S(2)}) %collective-permute-start.13) | collective-permute-done | bytes 524320 | tf_op jit(solution)/shard_map/ppermute | solution.py:47
  60.7 1.3 %fusion.8 = (f32[512,256]{1,0:T(8,128)S(1)}, f32[512,256]{1,0:T(8,128)S(1)}) fusion(f32[1024,256]{1,0:T(8,128)} %get-tuple-element.42, f32[512,256]{1,0:T(8,128)S(1)} %collective-permute-done.13), kind=kLoop, calls=%fused_computation.38 | loop fusion | flops 131072 | bytes 2621440 | tf_op jit(solution)/shard_map/slice | solution.py:245
  62.2 4.1 %collective-permute-done.4.refs_1_ = bf16[1024,256]{1,0:T(8,128)(2,1)S(1)} collective-permute-done((bf16[1024,256]{1,0:T(8,128)(2,1)S(1)}, bf16[1024,256]{1,0:T(8,128)(2,1)S(1)}, u32[]{:S(2)}, u32[]{:S(2)}) %collective-permute-start.4) | collective-permute-done | bytes 524320 | tf_op jit(solution)/shard_map/ppermute | solution.py:47
  66.3 3.0 %fused.8 = (f32[512,256]{1,0:T(8,128)S(1)}, f32[256,2048]{1,0:T(8,128)S(1)}, f32[8,2048]{1,0:T(8,128)S(1)}) custom-call(s32[3]{0:T(128)S(1)} %pad_add_fusion.refs_0_, bf16[1024,256]{1,0:T(8,128)(2,1)S(1)} %collective-permute-done.4.refs_1_, bf16[2048,256]{1,0:T(8,128)(2,1)S(1)} %get-tuple-element.24.refs_2_, ...), custom_call_target="tpu_custom_call", output_to_operand_aliasing={{1}: (8, {})} | custom-call | flops 1610612736 | bytes 8388608 | tf_op jit(solution)/shard_map/fused/pallas_call | solution.py:185
  69.3 3.0 %fused.9 = (f32[520,256]{1,0:T(8,128)S(1)}, f32[256,2048]{1,0:T(8,128)S(1)}, f32[8,256]{1,0:T(8,128)S(1)}) custom-call(s32[3]{0:T(128)S(1)} %pad_add_fusion.refs_0_, bf16[1024,256]{1,0:T(8,128)(2,1)S(1)} %collective-permute-done.4.refs_1_, bf16[2048,256]{1,0:T(8,128)(2,1)S(1)} %get-tuple-element.24.refs_2_, ...), custom_call_target="tpu_custom_call", output_to_operand_aliasing={{1}: (8, {})} | custom-call | flops 1610612736 | bytes 8388608 | tf_op jit(solution)/shard_map/fused/pallas_call | solution.py:185
  72.4 0.1 collective-permute-start.12
  72.6 1.5 %collective-permute-start.15 = (f32[8,256]{1,0:T(8,128)S(1)}, f32[8,256]{1,0:T(8,128)S(1)}, u32[]{:S(2)}, u32[]{:S(2)}) collective-permute-start(f32[8,256]{1,0:T(8,128)S(1)} %get-tuple-element.44), channel_id=1, source_target_pairs={{0,1},{2,3},{4,5},{6,7},{8,10},{10,12},{12,14},{14,8},{1,16},{3,18... | collective-permute-start | bytes 24584 | tf_op jit(solution)/shard_map/ppermute | solution.py:47
  74.1 1.7 %collective-permute-start.16 = (f32[8,256]{1,0:T(8,128)S(1)}, f32[8,256]{1,0:T(8,128)S(1)}, u32[]{:S(2)}, u32[]{:S(2)}) collective-permute-start(f32[8,256]{1,0:T(8,128)S(1)} %get-tuple-element.44), channel_id=1, source_target_pairs={{0,16},{2,18},{4,20},{6,22},{8,12},{10,14},{12,8},{14,10},{1,17},{... | collective-permute-start | bytes 24584 | tf_op jit(solution)/shard_map/ppermute | solution.py:47
  75.8 5.0 %collective-permute-done.12 = f32[520,256]{1,0:T(8,128)S(1)} collective-permute-done((f32[520,256]{1,0:T(8,128)S(1)}, f32[520,256]{1,0:T(8,128)S(1)}, u32[]{:S(2)}, u32[]{:S(2)}) %collective-permute-start.12) | collective-permute-done | bytes 532512 | tf_op jit(solution)/shard_map/ppermute | solution.py:47
  80.9 5.5 %collective-permute-done.11 = f32[512,256]{1,0:T(8,128)S(1)} collective-permute-done((f32[512,256]{1,0:T(8,128)S(1)}, f32[512,256]{1,0:T(8,128)S(1)}, u32[]{:S(2)}, u32[]{:S(2)}) %collective-permute-start.11) | collective-permute-done | bytes 524320 | tf_op jit(solution)/shard_map/ppermute | solution.py:47
  86.5 0.2 fusion
  86.8 0.6 collective-permute-start.17
  87.5 0.9 collective-permute-start.18
  88.4 0.4 collective-permute-start.19
  88.7 3.8 %collective-permute-done.17 = f32[264,256]{1,0:T(8,128)S(1)} collective-permute-done((f32[264,256]{1,0:T(8,128)S(1)}, f32[264,256]{1,0:T(8,128)S(1)}, u32[]{:S(2)}, u32[]{:S(2)}) %collective-permute-start.17) | collective-permute-done | bytes 270368 | tf_op jit(solution)/shard_map/ppermute | solution.py:47
  92.5 4.7 %collective-permute-done.18 = f32[264,256]{1,0:T(8,128)S(1)} collective-permute-done((f32[264,256]{1,0:T(8,128)S(1)}, f32[264,256]{1,0:T(8,128)S(1)}, u32[]{:S(2)}, u32[]{:S(2)}) %collective-permute-start.18) | collective-permute-done | bytes 270368 | tf_op jit(solution)/shard_map/ppermute | solution.py:47
  97.2 0.1 fusion.4
  97.3 3.5 %collective-permute-start.20 = (f32[136,256]{1,0:T(8,128)S(1)}, f32[136,256]{1,0:T(8,128)S(1)}, u32[]{:S(2)}, u32[]{:S(2)}) collective-permute-start(f32[136,256]{1,0:T(8,128)S(1)} %slice.102), channel_id=1, source_target_pairs={{0,8},{8,0},{1,9},{9,1},{2,10},{10,2},{3,11},{11,3},{4,12},{12,4},... | collective-permute-start | bytes 417800 | tf_op jit(solution)/shard_map/ppermute | solution.py:30
  100.8 1.1 slice.73
  102.0 0.7 pad_maximum_fusion.5
  102.7 3.4 %all-to-all-start.1 = ((f32[8,72,128]{2,1,0:T(8,128)}), f32[8,72,128]{2,1,0:T(8,128)S(1)}, u32[]{:S(2)}, u32[]{:S(2)}) async-start(f32[8,72,128]{2,1,0:T(8,128)} %pad_maximum_fusion.5), calls=%async_computation.1 | async-start | bytes 589824 | tf_op jit(solution)/shard_map/all_to_all | solution.py:265
  106.2 1.4 %fusion.1 = bf16[1024,256]{0,1:T(8,128)(2,1)S(1)} fusion(f32[256,1024]{1,0:T(8,128)} %collective-permute-done.9, f32[256,2048]{1,0:T(8,128)S(1)} %get-tuple-element.37), kind=kLoop, calls=%fused_computation.8 | loop fusion | flops 786432 | bytes 2621440 | tf_op jit(solution)/shard_map/convert_element_type | solution.py:273
  107.6 1.0 copy.13
  108.6 10.4 %all-to-all-done.1 = f32[8,72,128]{2,1,0:T(8,128)S(1)} async-done(((f32[8,72,128]{2,1,0:T(8,128)}), f32[8,72,128]{2,1,0:T(8,128)S(1)}, u32[]{:S(2)}, u32[]{:S(2)}) %all-to-all-start.1) | async-done | bytes 294944 | tf_op jit(solution)/shard_map/all_to_all | solution.py:265
  119.1 0.6 fusion.6
  119.7 0.6 slice_reduce_fusion.1
  (42 shorter events, 0.9 us)
Async XLA Ops:
  2.0 16.8 %all-to-all-start = ((bf16[8,32,256]{2,1,0:T(8,128)(2,1)}), bf16[8,32,256]{2,1,0:T(8,128)(2,1)S(1)}, u32[]{:S(2)}, u32[]{:S(2)}) async-start(bf16[8,32,256]{2,1,0:T(8,128)(2,1)} %broadcast_in_dim.6), calls=%async_computation | async-start | bytes 262144 | tf_op jit(solution)/shard_map/all_to_all | solution.py:223
  18.8 3.3 %collective-permute-start = (bf16[128,256]{1,0:T(8,128)(2,1)S(1)}, bf16[128,256]{1,0:T(8,128)(2,1)S(1)}, u32[]{:S(2)}, u32[]{:S(2)}) collective-permute-start(bf16[128,256]{1,0:T(8,128)(2,1)S(1)} %bitcast.22), channel_id=1, source_target_pairs={{0,8},{8,0},{1,9},{9,1},{2,10},{10,2},{3,11},{11,3},{4,12},{12,4},... | collective-permute-start | bytes 196616 | tf_op jit(solution)/shard_map/ppermute | solution.py:30
  21.2 17.6 %collective-permute-start.5 = (bf16[1024,256]{1,0:T(8,128)(2,1)}, bf16[1024,256]{1,0:T(8,128)(2,1)S(1)}, u32[]{:S(2)}, u32[]{:S(2)}) collective-permute-start(bf16[1024,256]{1,0:T(8,128)(2,1)} %refs_2_.1), channel_id=1, source_target_pairs={{0,8},{8,0},{1,9},{9,1},{2,10},{10,2},{3,11},{11,3},{4,12},{12,4},... | collective-permute-start | bytes 1572872 | tf_op jit(solution)/shard_map/ppermute | solution.py:30
  22.1 5.4 %collective-permute-start.1 = (bf16[256,256]{1,0:T(8,128)(2,1)S(1)}, bf16[256,256]{1,0:T(8,128)(2,1)S(1)}, u32[]{:S(2)}, u32[]{:S(2)}) collective-permute-start(bf16[256,256]{1,0:T(8,128)(2,1)S(1)} %pad_maximum_fusion.7), channel_id=1, source_target_pairs={{0,2},{2,4},{4,6},{6,0},{8,9},{10,11},{12,13},{14,15},{1,3},{3,5},... | collective-permute-start | bytes 393224 | tf_op jit(solution)/shard_map/ppermute | solution.py:47
  23.4 4.1 %collective-permute-start.2 = (bf16[256,256]{1,0:T(8,128)(2,1)S(1)}, bf16[256,256]{1,0:T(8,128)(2,1)S(1)}, u32[]{:S(2)}, u32[]{:S(2)}) collective-permute-start(bf16[256,256]{1,0:T(8,128)(2,1)S(1)} %pad_maximum_fusion.7), channel_id=1, source_target_pairs={{0,6},{2,0},{4,2},{6,4},{8,25},{10,27},{12,29},{14,31},{1,7},{3,1}... | collective-permute-start | bytes 393224 | tf_op jit(solution)/shard_map/ppermute | solution.py:47
  24.8 5.6 %collective-permute-start.3 = (bf16[256,256]{1,0:T(8,128)(2,1)S(1)}, bf16[256,256]{1,0:T(8,128)(2,1)S(1)}, u32[]{:S(2)}, u32[]{:S(2)}) collective-permute-start(bf16[256,256]{1,0:T(8,128)(2,1)S(1)} %pad_maximum_fusion.7), channel_id=1, source_target_pairs={{0,4},{2,6},{4,0},{6,2},{8,24},{10,26},{12,28},{14,30},{1,5},{3,7}... | collective-permute-start | bytes 393224 | tf_op jit(solution)/shard_map/ppermute | solution.py:47
  30.5 14.5 %collective-permute-start.8 = (bf16[1024,256]{1,0:T(8,128)(2,1)S(1)}, bf16[1024,256]{1,0:T(8,128)(2,1)}, u32[]{:S(2)}, u32[]{:S(2)}) collective-permute-start(bf16[1024,256]{1,0:T(8,128)(2,1)S(1)} %constant_dynamic-update-slice_fusion.refs_1_), channel_id=1, source_target_pairs={{0,16},{2,18},{4,20},{6,22},{8,12},{10,14},{12,8},{14,10},{1,17},{... | collective-permute-start | bytes 1572872 | tf_op jit(solution)/shard_map/ppermute | solution.py:47
  33.9 4.8 %collective-permute-start.6 = (f32[3,1024]{1,0:T(4,128)S(1)}, f32[3,1024]{1,0:T(4,128)S(1)}, u32[]{:S(2)}, u32[]{:S(2)}) collective-permute-start(f32[3,1024]{1,0:T(4,128)S(1)} %pad_maximum_fusion.8.refs_4_), channel_id=1, source_target_pairs={{0,8},{8,0},{1,9},{9,1},{2,10},{10,2},{3,11},{11,3},{4,12},{12,4},... | collective-permute-start | bytes 36872 | tf_op jit(solution)/shard_map/ppermute | solution.py:30
  37.0 16.7 %collective-permute-start.7 = (bf16[1024,256]{1,0:T(8,128)(2,1)S(1)}, bf16[1024,256]{1,0:T(8,128)(2,1)S(1)}, u32[]{:S(2)}, u32[]{:S(2)}) collective-permute-start(bf16[1024,256]{1,0:T(8,128)(2,1)S(1)} %constant_dynamic-update-slice_fusion.refs_1_), channel_id=1, source_target_pairs={{0,17},{2,19},{4,21},{6,23},{8,14},{10,8},{12,10},{14,12},{1,0},{3... | collective-permute-start | bytes 1572872 | tf_op jit(solution)/shard_map/ppermute | solution.py:47
  50.9 9.8 %collective-permute-start.13 = (f32[512,256]{1,0:T(8,128)}, f32[512,256]{1,0:T(8,128)S(1)}, u32[]{:S(2)}, u32[]{:S(2)}) collective-permute-start(f32[512,256]{1,0:T(8,128)} %get-tuple-element.43), channel_id=1, source_target_pairs={{0,1},{2,3},{4,5},{6,7},{8,10},{10,12},{12,14},{14,8},{1,16},{3,18... | collective-permute-start | bytes 1572872 | tf_op jit(solution)/shard_map/ppermute | solution.py:47
  51.0 15.4 %collective-permute-start.4 = (bf16[1024,256]{1,0:T(8,128)(2,1)S(1)}, bf16[1024,256]{1,0:T(8,128)(2,1)S(1)}, u32[]{:S(2)}, u32[]{:S(2)}) collective-permute-start(bf16[1024,256]{1,0:T(8,128)(2,1)S(1)} %constant_dynamic-update-slice_fusion.refs_1_), channel_id=1, source_target_pairs={{0,1},{2,3},{4,5},{6,7},{8,10},{10,12},{12,14},{14,8},{1,16},{3,18... | collective-permute-start | bytes 1572872 | tf_op jit(solution)/shard_map/ppermute | solution.py:47
  51.1 21.3 %collective-permute-start.10 = (f32[512,256]{1,0:T(8,128)}, f32[512,256]{1,0:T(8,128)S(1)}, u32[]{:S(2)}, u32[]{:S(2)}) collective-permute-start(f32[512,256]{1,0:T(8,128)} %get-tuple-element.40), channel_id=1, source_target_pairs={{0,17},{2,19},{4,21},{6,23},{8,14},{10,8},{12,10},{14,12},{1,0},{3... | collective-permute-start | bytes 1572872 | tf_op jit(solution)/shard_map/ppermute | solution.py:47
  62.1 24.4 %collective-permute-start.14 = (f32[1024,256]{1,0:T(8,128)S(1)}, f32[1024,256]{1,0:T(8,128)S(1)}, u32[]{:S(2)}, u32[]{:S(2)}) collective-permute-start(f32[1024,256]{1,0:T(8,128)S(1)} %pad_maximum_fusion), channel_id=1, source_target_pairs={{0,1},{2,3},{4,5},{6,7},{8,10},{10,12},{12,14},{14,8},{1,16},{3,18... | collective-permute-start | bytes 3145736 | tf_op jit(solution)/shard_map/ppermute | solution.py:47
  72.3 14.1 %copy-start = (f32[1024,256]{1,0:T(8,128)S(1)}, f32[1024,256]{1,0:T(8,128)}, u32[]{:S(2)}) copy-start(f32[1024,256]{1,0:T(8,128)} %get-tuple-element.38) | copy-start | bytes 3145732
  72.4 8.5 %collective-permute-start.12 = (f32[520,256]{1,0:T(8,128)S(1)}, f32[520,256]{1,0:T(8,128)S(1)}, u32[]{:S(2)}, u32[]{:S(2)}) collective-permute-start(f32[520,256]{1,0:T(8,128)S(1)} %get-tuple-element.41), channel_id=1, source_target_pairs={{0,17},{2,19},{4,21},{6,23},{8,14},{10,8},{12,10},{14,12},{1,0},{3... | collective-permute-start | bytes 1597448 | tf_op jit(solution)/shard_map/ppermute | solution.py:47
  72.5 13.9 %collective-permute-start.11 = (f32[512,256]{1,0:T(8,128)S(1)}, f32[512,256]{1,0:T(8,128)S(1)}, u32[]{:S(2)}, u32[]{:S(2)}) collective-permute-start(f32[512,256]{1,0:T(8,128)S(1)} %add.44), channel_id=1, source_target_pairs={{0,17},{2,19},{4,21},{6,23},{8,14},{10,8},{12,10},{14,12},{1,0},{3... | collective-permute-start | bytes 1572872 | tf_op jit(solution)/shard_map/ppermute | solution.py:47
  72.6 8.3 %collective-permute-start.15 = (f32[8,256]{1,0:T(8,128)S(1)}, f32[8,256]{1,0:T(8,128)S(1)}, u32[]{:S(2)}, u32[]{:S(2)}) collective-permute-start(f32[8,256]{1,0:T(8,128)S(1)} %get-tuple-element.44), channel_id=1, source_target_pairs={{0,1},{2,3},{4,5},{6,7},{8,10},{10,12},{12,14},{14,8},{1,16},{3,18... | collective-permute-start | bytes 24584 | tf_op jit(solution)/shard_map/ppermute | solution.py:47
  74.1 6.8 %collective-permute-start.16 = (f32[8,256]{1,0:T(8,128)S(1)}, f32[8,256]{1,0:T(8,128)S(1)}, u32[]{:S(2)}, u32[]{:S(2)}) collective-permute-start(f32[8,256]{1,0:T(8,128)S(1)} %get-tuple-element.44), channel_id=1, source_target_pairs={{0,16},{2,18},{4,20},{6,22},{8,12},{10,14},{12,8},{14,10},{1,17},{... | collective-permute-start | bytes 24584 | tf_op jit(solution)/shard_map/ppermute | solution.py:47
  86.8 5.7 %collective-permute-start.17 = (f32[264,256]{1,0:T(8,128)S(1)}, f32[264,256]{1,0:T(8,128)S(1)}, u32[]{:S(2)}, u32[]{:S(2)}) collective-permute-start(f32[264,256]{1,0:T(8,128)S(1)} %get-tuple-element.65), channel_id=1, source_target_pairs={{0,6},{2,0},{4,2},{6,4},{8,25},{10,27},{12,29},{14,31},{1,7},{3,1}... | collective-permute-start | bytes 811016 | tf_op jit(solution)/shard_map/ppermute | solution.py:47
  87.5 9.7 %collective-permute-start.18 = (f32[264,256]{1,0:T(8,128)S(1)}, f32[264,256]{1,0:T(8,128)S(1)}, u32[]{:S(2)}, u32[]{:S(2)}) collective-permute-start(f32[264,256]{1,0:T(8,128)S(1)} %get-tuple-element.66), channel_id=1, source_target_pairs={{0,2},{2,4},{4,6},{6,0},{8,9},{10,11},{12,13},{14,15},{1,3},{3,5},... | collective-permute-start | bytes 811016 | tf_op jit(solution)/shard_map/ppermute | solution.py:47
  88.4 8.8 %collective-permute-start.19 = (f32[264,256]{1,0:T(8,128)S(1)}, f32[264,256]{1,0:T(8,128)S(1)}, u32[]{:S(2)}, u32[]{:S(2)}) collective-permute-start(f32[264,256]{1,0:T(8,128)S(1)} %get-tuple-element.67), channel_id=1, source_target_pairs={{0,4},{2,6},{4,0},{6,2},{8,24},{10,26},{12,28},{14,30},{1,5},{3,7}... | collective-permute-start | bytes 811016 | tf_op jit(solution)/shard_map/ppermute | solution.py:47
  97.3 4.6 %collective-permute-start.20 = (f32[136,256]{1,0:T(8,128)S(1)}, f32[136,256]{1,0:T(8,128)S(1)}, u32[]{:S(2)}, u32[]{:S(2)}) collective-permute-start(f32[136,256]{1,0:T(8,128)S(1)} %slice.102), channel_id=1, source_target_pairs={{0,8},{8,0},{1,9},{9,1},{2,10},{10,2},{3,11},{11,3},{4,12},{12,4},... | collective-permute-start | bytes 417800 | tf_op jit(solution)/shard_map/ppermute | solution.py:30
  101.9 4.3 %collective-permute-start.9 = (f32[256,1024]{1,0:T(8,128)}, f32[256,1024]{1,0:T(8,128)}, u32[]{:S(2)}, u32[]{:S(2)}) collective-permute-start(f32[256,1024]{1,0:T(8,128)} %slice.73), channel_id=1, source_target_pairs={{0,8},{8,0},{1,9},{9,1},{2,10},{10,2},{3,11},{11,3},{4,12},{12,4},... | collective-permute-start | bytes 3145736 | tf_op jit(solution)/shard_map/ppermute | solution.py:30
  102.7 16.3 %all-to-all-start.1 = ((f32[8,72,128]{2,1,0:T(8,128)}), f32[8,72,128]{2,1,0:T(8,128)S(1)}, u32[]{:S(2)}, u32[]{:S(2)}) async-start(f32[8,72,128]{2,1,0:T(8,128)} %pad_maximum_fusion.5), calls=%async_computation.1 | async-start | bytes 589824 | tf_op jit(solution)/shard_map/all_to_all | solution.py:265
